TPU v7x, 32 devices: a whole 2x2x4 slice. The times are simulated.
32 devices in a mesh: client: 8 (over z, x), head: 4 (over y, core).
Axes of the slice: x: 2, y: 2, z: 4, core: 2. Of those that a mesh axis runs over, the one named last changes fastest.
Arguments:
- pre: bfloat16 [10240, 4096], P('client'), may hold values from -40 to 40
- delta: float32 [10240, 4096], P('client', 'head'), may hold values from -300 to 300
- head_weight: bfloat16 [4096, 4096], P(None, 'head'), may hold values from -0.09375 to 0.09375
- client_ids: int32 [128], P('client'), may hold values from 0 to 127, as said below
Outputs:
- head_grad: float32 [4096, 4096], P('client', 'head')
- bias_grad: float32 [4096], P('head')
- embed_grad: float32 [128, 4096], P('client', 'head')
- span_grad: float32 [80, 4096], P(None, 'head')
Inputs may be any that keep to these rules, and one draw needn't show every extreme that they name: `client_ids`: each of the 128 clients appears exactly once.
All inputs are finite; a program needn't handle non-finite values.
Results may differ from a plain program's by a relative error of at most 0.024.
Values may be sent and summed in bfloat16 or wider, within the bound.
A program may use at most 128 MiB of HBM per device.

v0:
```python
import functools

import jax
import jax.numpy as jnp
from jax import lax
from jax.experimental import pallas as pl
from jax.experimental.pallas import tpu as pltpu
from jax.sharding import PartitionSpec as P

EPSILON = 1e-06
MESH = pl.DeviceIdType.MESH
F32 = jnp.float32
BF16 = jnp.bfloat16


def clip_factor(total, number):
    return jnp.minimum(1.0, 1.0 / jnp.sqrt(total / number + EPSILON))


def flip(index, mask, bits):
    out = 0
    for b in range(bits):
        i = (index // 2**b) % 2
        m = (mask // 2**b) % 2
        out = out + (i + m - 2 * i * m) * 2**b
    return out


def kernel(cfg, pre_ref, delta_ref, weight_ref, ids_ref, head_out, rest_out, embed_out, stat_out,
           pre_v, delta_v, low, weight_v, part, landed, small, small_in, mine, span_in, span_all,
           embed_all, ids_all, stat, stat_in, stat_head_in,
           pre_sem, delta_sem, weight_sem, tree_send, tree_recv, head_send, head_recv,
           span_send, span_recv, gather_send, gather_recv, embed_send, embed_recv,
           ids_send, ids_recv, stat_send, stat_recv):
    n, heads, q, piece, groups, spans, clients = cfg
    bits = n.bit_length() - 1
    block = q * piece
    half = n // 2 * q
    pieces = n * q
    me = lax.axis_index("client")
    my_head = lax.axis_index("head")
    emit = low.shape[1]

    barrier = pltpu.get_barrier_semaphore()
    for d in range(1, n):
        pl.semaphore_signal(barrier, inc=1, device_id={"client": lax.rem(me + d, n)}, device_id_type=MESH)
    for d in range(1, heads):
        pl.semaphore_signal(barrier, inc=1, device_id={"head": lax.rem(my_head + d, heads)}, device_id_type=MESH)

    def place(i):
        pos = i // q
        upper = pos // (n // 2)
        mask = n - 2 - 2 * (pos % (n // 2)) + 1 - upper
        row = flip(me, mask, bits) * block + (i % q) * piece
        return pl.multiple_of(row, piece)

    def pre_copy(i):
        return pltpu.make_async_copy(pre_ref.at[:, pl.ds(place(i), piece)], pre_v.at[i], pre_sem.at[i])

    delta_copy = pltpu.make_async_copy(delta_ref, delta_v, delta_sem)
    weight_copy = pltpu.make_async_copy(weight_ref, weight_v, weight_sem)
    delta_copy.start()
    ahead = 3
    for i in range(ahead):
        pre_copy(i).start()

    delta_copy.wait()
    step = 64
    def narrow(r, total):
        rows = pl.ds(pl.multiple_of(r * step, step), step)
        x = delta_v[rows, :]
        low[rows, :] = x.astype(BF16)
        return total + jnp.sum(x.reshape(step // 8, 8, emit), axis=0)
    bias = lax.fori_loop(0, low.shape[0] // step, narrow, jnp.zeros((8, emit), F32))
    bias = jnp.sum(bias, axis=0, keepdims=True)
    pad = groups * 16 - spans
    mine[pl.ds(spans, pad), :] = jnp.where(
        lax.broadcasted_iota(jnp.int32, (pad, emit), 0) == 0, jnp.broadcast_to(bias, (pad, emit)), 0.0
    ).astype(BF16)

    pl.semaphore_wait(barrier, n - 1 + heads - 1)

    def product(i):
        pre_copy(i).wait()
        p = pre_v[i].astype(F32)
        hidden = (p * jax.nn.sigmoid(p)).astype(BF16)
        value = lax.dot_general(hidden, low[...], (((0,), (0,)), ((), ())), preferred_element_type=F32)
        part[pl.ds(place(i), piece), :] = value.astype(BF16)

    def tree_copy(source_row, slot, stage):
        return pltpu.make_async_remote_copy(
            src_ref=part.at[pl.ds(source_row, piece), :], dst_ref=landed.at[slot],
            send_sem=tree_send.at[slot], recv_sem=tree_recv.at[slot],
            device_id={"client": flip(me, 2**stage, bits)}, device_id_type=MESH)

    def first_slot(i):
        return (n // 2 - 1 - i // q) * q + i % q

    def first(i, carry):
        pre_copy(i + ahead).start()
        product(i)
        tree_copy(place(i), first_slot(i), 0).start()
        return carry
    lax.fori_loop(0, half, first, 0)
    weight_copy.start()

    ids_copies = []
    for d in range(1, n):
        copy = pltpu.make_async_remote_copy(
            src_ref=ids_ref, dst_ref=ids_all.at[d],
            send_sem=ids_send.at[d], recv_sem=ids_recv.at[d],
            device_id={"client": lax.rem(me + d, n)}, device_id_type=MESH)
        copy.start()
        ids_copies.append(copy)

    def own(i, carry):
        @pl.when(i + ahead < pieces)
        def _():
            pre_copy(i + ahead).start()
        product(i)
        return carry
    lax.fori_loop(half, pieces, own, 0)
    weight_copy.wait()

    def slope_sums(i, carry):
        p = pre_v[i].astype(F32)
        row = place(i)
        value = lax.dot_general(
            low[...], weight_v[pl.ds(row, piece), :], (((1,), (1,)), ((), ())), preferred_element_type=F32)
        s = jax.nn.sigmoid(p)
        grad = value.astype(BF16).astype(F32) * (s * (1.0 + p * (1.0 - s)))
        grad = grad.reshape(clients, spans, piece)
        to = row // emit
        columns = pl.ds(pl.multiple_of(row % emit, piece), piece)
        small[to, pl.ds(0, spans), columns] = jnp.sum(grad, axis=0).astype(BF16)
        small[to, pl.ds(spans, clients), columns] = jnp.sum(grad, axis=1).astype(BF16)
        return carry

    bases = [0]
    for s in range(bits):
        bases.append(bases[-1] + (n >> (s + 1)) * q)
    later = []

    def combine(mask, sub):
        row = pl.multiple_of(flip(me, mask, bits) * block + sub * piece, piece)
        level = bits if mask == 0 else (mask & -mask).bit_length() - 1
        for s in range(level):
            slot = bases[s] + (mask >> (s + 1)) * q + sub
            tree_copy(row, slot, s).wait_recv()
        def chunk(r, carry):
            rows = min(64, piece)
            at = pl.multiple_of(r * rows, rows)
            total = part[pl.ds(pl.multiple_of(row + at, rows), rows), :].astype(F32)
            for s in range(level):
                slot = bases[s] + (mask >> (s + 1)) * q + sub
                total = total + landed[slot, pl.ds(at, rows), :].astype(F32)
            if mask == 0:
                head_out[pl.ds(pl.multiple_of(sub * piece + at, rows), rows), :] = total
                return carry + jnp.sum((total * total).reshape(rows // 8, 8, emit), axis=0)
            part[pl.ds(pl.multiple_of(row + at, rows), rows), :] = total.astype(BF16)
            return carry
        rows = min(64, piece)
        start = jnp.zeros((8, emit), F32)
        total = lax.fori_loop(0, piece // rows, chunk, start if mask == 0 else 0)
        if mask == 0:
            return total
        slot = bases[level] + (mask >> (level + 1)) * q + sub
        copy = tree_copy(row, slot, level)
        copy.start()
        later.append(copy)

    order = [(mask, sub) for mask in range(n - 2, -1, -2) for sub in range(q)]
    before = order[: 3 * len(order) // 8]
    middle = order[len(before): 3 * len(order) // 4]
    last = order[len(before) + len(middle):]
    for item in before:
        combine(*item)
    at = 0
    for k, item in enumerate(middle):
        upto = pieces * (k + 1) // len(middle)
        lax.fori_loop(at, upto, slope_sums, 0)
        at = upto
        if k == len(middle) - 1:
            head_copies = []
            for d in range(1, heads):
                target = lax.rem(my_head + d, heads)
                copy = pltpu.make_async_remote_copy(
                    src_ref=small.at[target], dst_ref=small_in.at[d - 1],
                    send_sem=head_send.at[d - 1], recv_sem=head_recv.at[d - 1],
                    device_id={"head": target}, device_id_type=MESH)
                copy.start()
                head_copies.append(copy)
        combine(*item)

    for copy in head_copies:
        copy.wait_recv()
    total = small[my_head].astype(F32)
    for d in range(heads - 1):
        total = total + small_in[d].astype(F32)
    mine[pl.ds(0, spans), :] = total[:spans].astype(BF16)
    embed_all[0] = total[spans:].astype(BF16)

    def span_copy(d):
        target = lax.rem(me + d, n)
        return target, pltpu.make_async_remote_copy(
            src_ref=mine.at[pl.ds(pl.multiple_of(lax.rem(target, groups) * 16, 16), 16), :],
            dst_ref=span_in.at[d], send_sem=span_send.at[d], recv_sem=span_recv.at[d],
            device_id={"client": target}, device_id_type=MESH)

    for d in range(1, n):
        target, copy = span_copy(d)
        @pl.when(target < groups)
        def _():
            copy.start()
    embed_copies = []
    for d in range(1, n):
        copy = pltpu.make_async_remote_copy(
            src_ref=embed_all.at[0], dst_ref=embed_all.at[d],
            send_sem=embed_send.at[d], recv_sem=embed_recv.at[d],
            device_id={"client": lax.rem(me + d, n)}, device_id_type=MESH)
        copy.start()
        embed_copies.append(copy)

    head_square = jnp.zeros((8, emit), F32)
    for item in last[: len(last) // 2]:
        value = combine(*item)
        head_square = head_square if value is None else head_square + value

    def gather_copy(d):
        slot = lax.rem(me, groups)
        return pltpu.make_async_remote_copy(
            src_ref=span_all.at[slot], dst_ref=span_all.at[slot],
            send_sem=gather_send.at[d], recv_sem=gather_recv.at[slot],
            device_id={"client": lax.rem(me + d, n)}, device_id_type=MESH)

    @pl.when(me < groups)
    def _():
        for d in range(1, n):
            span_copy(d)[1].wait_recv()
        total = mine[pl.ds(pl.multiple_of(lax.rem(me, groups) * 16, 16), 16), :].astype(F32)
        for d in range(1, n):
            total = total + span_in[d].astype(F32)
        span_all[lax.rem(me, groups)] = total.astype(BF16)
        for d in range(1, n):
            gather_copy(d).start()

    for copy in embed_copies + ids_copies:
        copy.wait_recv()
    wanted = lax.broadcasted_iota(jnp.int32, (clients, 128), 1) + me * clients
    embed_raw = jnp.zeros((clients, emit), F32)
    for d in range(n):
        ids = ids_ref[...] if d == 0 else ids_all[d]
        chosen = (ids == wanted).astype(F32).astype(BF16)
        picked = lax.dot_general(chosen, embed_all[d], (((0,), (0,)), ((), ())), preferred_element_type=F32)
        embed_raw = embed_raw + picked[:clients]
    embed_out[...] = embed_raw
    embed_square = jnp.sum(embed_raw * embed_raw)

    for g in range(groups):
        @pl.when(me != g)
        def _():
            pltpu.make_async_remote_copy(
                src_ref=span_all.at[g], dst_ref=span_all.at[g],
                send_sem=gather_send.at[0], recv_sem=gather_recv.at[g],
                device_id={"client": lax.rem(me + 1, n)}, device_id_type=MESH).wait_recv()
    rest_square = jnp.zeros((), F32)
    for g in range(groups):
        value = span_all[g].astype(F32)
        rest_out[pl.ds(16 * g, 16), :] = value
        rest_square = rest_square + jnp.sum(value * value)

    for item in last[len(last) // 2:]:
        value = combine(*item)
        head_square = head_square if value is None else head_square + value
    head_total = jnp.sum(head_square)

    line = lax.broadcasted_iota(jnp.int32, (8, 128), 0)
    stat[0] = jnp.where(line == 0, head_total, jnp.where(line == 1, embed_square, rest_square / n))
    copies = []
    for d in range(1, n):
        copy = pltpu.make_async_remote_copy(
            src_ref=stat.at[0], dst_ref=stat_in.at[d - 1], send_sem=stat_send.at[d - 1],
            recv_sem=stat_recv.at[d - 1], device_id={"client": lax.rem(me + d, n)}, device_id_type=MESH)
        copy.start()
        copies.append(copy)
    total = stat[0]
    for d, copy in enumerate(copies):
        copy.wait_recv()
        total = total + stat_in[d]
    stat[1] = total
    more = []
    for d in range(1, heads):
        slot = n - 2 + d
        copy = pltpu.make_async_remote_copy(
            src_ref=stat.at[1], dst_ref=stat_head_in.at[d - 1], send_sem=stat_send.at[slot],
            recv_sem=stat_recv.at[slot], device_id={"head": lax.rem(my_head + d, heads)}, device_id_type=MESH)
        copy.start()
        more.append(copy)
    for d, copy in enumerate(more):
        copy.wait_recv()
        total = total + stat_head_in[d]
    stat_out[...] = total

    def sent(i, carry):
        tree_copy(place(i), first_slot(i), 0).wait_send()
        return carry
    lax.fori_loop(0, half, sent, 0)
    for copy in later + head_copies + embed_copies + ids_copies + copies + more:
        copy.wait_send()
    for d in range(1, n):
        target, copy = span_copy(d)
        @pl.when(target < groups)
        def _():
            copy.wait_send()
    @pl.when(me < groups)
    def _():
        for d in range(1, n):
            gather_copy(d).wait_send()


def per_device(n, heads, pre, delta, head_weight, client_ids):
    rows, hidden_width = pre.shape
    emit = delta.shape[1]
    clients = client_ids.shape[0]
    spans = rows // clients
    block = hidden_width // n
    piece = min(256, block)
    q = block // piece
    groups = (spans + 16) // 16
    cfg = (n, heads, q, piece, groups, spans, clients)
    ids = jnp.broadcast_to(client_ids[:, None], (clients, 128))
    hbm = pl.BlockSpec(memory_space=pl.ANY)
    vmem = pl.BlockSpec(memory_space=pltpu.VMEM)
    dma = pltpu.SemaphoreType.DMA
    slots = (n - 1) * q
    head_raw, rest_raw, embed_raw, stats = pl.pallas_call(
        functools.partial(kernel, cfg),
        out_shape=(
            jax.ShapeDtypeStruct((block, emit), F32),
            jax.ShapeDtypeStruct((groups * 16, emit), F32),
            jax.ShapeDtypeStruct((clients, emit), F32),
            jax.ShapeDtypeStruct((8, 128), F32),
        ),
        in_specs=[hbm, hbm, hbm, vmem],
        out_specs=(vmem, vmem, vmem, vmem),
        scratch_shapes=[
            pltpu.VMEM((n * q, rows, piece), BF16),
            pltpu.VMEM((rows, emit), F32),
            pltpu.VMEM((rows, emit), BF16),
            pltpu.VMEM((hidden_width, emit), BF16),
            pltpu.VMEM((hidden_width, emit), BF16),
            pltpu.VMEM((slots, piece, emit), BF16),
            pltpu.VMEM((heads, spans + clients, emit), BF16),
            pltpu.VMEM((heads - 1, spans + clients, emit), BF16),
            pltpu.VMEM((groups * 16, emit), BF16),
            pltpu.VMEM((n, 16, emit), BF16),
            pltpu.VMEM((groups, 16, emit), BF16),
            pltpu.VMEM((n, clients, emit), BF16),
            pltpu.VMEM((n, clients, 128), jnp.int32),
            pltpu.VMEM((2, 8, 128), F32),
            pltpu.VMEM((n - 1, 8, 128), F32),
            pltpu.VMEM((heads - 1, 8, 128), F32),
            dma((n * q,)), dma, dma, dma((slots,)), dma((slots,)),
            dma((heads - 1,)), dma((heads - 1,)),
            dma((n,)), dma((n,)), dma((n,)), dma((groups,)), dma((n,)), dma((n,)),
            dma((n,)), dma((n,)), dma((n + heads - 2,)), dma((n + heads - 2,)),
        ],
        compiler_params=pltpu.CompilerParams(
            collective_id=0, has_side_effects=True, vmem_limit_bytes=60 * 2**20
        ),
        name="clipped_grads",
    )(pre, delta, head_weight, ids)
    head_factor = clip_factor(stats[0, 0], hidden_width * emit * heads)
    embed_factor = clip_factor(stats[1, 0], clients * n * hidden_width)
    rest_factor = clip_factor(stats[2, 0], spans * hidden_width + emit * heads)
    return (
        head_factor * head_raw,
        rest_factor * rest_raw[spans],
        embed_factor * embed_raw,
        rest_factor * rest_raw[:spans],
    )


def solution(mesh):
    placed = (P("client", None), P("client", "head"), P(None, "head"), P("client"))
    return jax.shard_map(
        functools.partial(per_device, mesh.shape["client"], mesh.shape["head"]),
        mesh=mesh,
        in_specs=placed,
        out_specs=(P("client", "head"), P("head"), P("client", "head"), P(None, "head")),
        check_vma=False,
    )
```

profile of v0, /device:TPU:0, one launch (start us, length us, event | category | flops | bytes accessed | tf_op | source)
XLA Modules:
  0.0 148.5 jit_solution(6204546828907031662)
XLA Ops:
  0.6 1.3 broadcast_in_dim.2.ids_ref
  2.0 135.4 %clipped_grads.1 = (f32[512,1024]{1,0:T(8,128)}, f32[96,1024]{1,0:T(8,128)}, f32[16,1024]{1,0:T(8,128)}, f32[8,128]{1,0:T(8,128)}) custom-call(bf16[1280,4096]{1,0:T(8,128)(2,1)} %pre_ref.1, f32[1280,1024]{1,0:T(8,128)} %delta_ref.1, bf16[4096,1024]{1,0:T(8,128)(2,1)} %weight_ref.1, s32[16,128]{1,0:T(8,128)} %broadcast_in_dim.2.ids_ref), custom_call_target="tpu_custom_call" | custom-call | tf_op jit(solution)/shard_map/clipped_grads/pallas_call | solution.py:336
  137.4 1.3 fusion
  139.4 1.7 %slice_multiply_fusion = f32[80,1024]{1,0:T(8,128)} fusion(f32[96,1024]{1,0:T(8,128)} %get-tuple-element.10, f32[]{:T(128)} %bitcast.1), kind=kLoop, calls=%fused_computation.1 | loop fusion | flops 81920 | bytes 655364 | tf_op jit(solution)/shard_map/mul | solution.py:380
  141.1 1.4 slice_multiply_fusion.1
  143.2 1.5 broadcast_multiply_fusion.1
  145.3 3.2 %broadcast_multiply_fusion = f32[512,1024]{1,0:T(8,128)} fusion(f32[512,1024]{1,0:T(8,128)} %get-tuple-element.9, f32[]{:T(128)} %bitcast), kind=kLoop, calls=%fused_computation | loop fusion | flops 524288 | bytes 4194308 | tf_op jit(solution)/shard_map/mul | solution.py:377
where the time goes:
time: 149 us
  Pallas kernels  135 us (91%)
  other arithmetic  7.76 us (5%)
  between operations  2.72 us (2%)
  local copies, waits for them, and re-layouts  2.62 us (2%)
    pallas_call x1, Pallas kernels, per_device(): pl.pallas_call(functools.partial(kernel, cfg), out_shape=(jax.ShapeDtypeS...  135 us
    mul x1, other arithmetic, per_device(): head_factor * head_raw  3.2 us

commit v1 on v0

v1 whole, which is shorter than its diff:
```python
import functools
import math

import jax
import jax.numpy as jnp
from jax import lax
from jax.experimental import pallas as pl
from jax.experimental.pallas import tpu as pltpu
from jax.sharding import PartitionSpec as P

EPSILON = 1e-06
MESH = pl.DeviceIdType.MESH
F32 = jnp.float32
BF16 = jnp.bfloat16


def clip_factor(total, number):
    return jnp.minimum(1.0, 1.0 / jnp.sqrt(total / number + EPSILON))


def kernel(cfg, pre_ref, delta_ref, weight_ref, ids_ref, head_out, rest_out, embed_out, stat_out,
           pre_v, delta_v, low, weight_v, part, pair_in, line_in, first_in, swap_in, head_v,
           small, small_in, mine, span_in, span_part, span_pair, span_all, embed_all, ids_all,
           stat, stat_in, stat_head_in,
           pre_sem, delta_sem, weight_sem, out_sem, pair_send, pair_recv, line_send, line_recv,
           first_send, first_recv, swap_sem, head_send, head_recv, span_send, span_recv, span_pair_sem,
           all_send, all_recv, embed_pair_sem, embed_send, embed_recv, ids_sem, ids_send, ids_recv,
           stat_send, stat_recv):
    n, heads, block, piece, spans, clients = cfg
    zs = n // 2
    q = 7
    sub = block // (q + 1)
    hq = block // piece
    rows, emit = low.shape
    me = lax.axis_index("client")
    my_head = lax.axis_index("head")
    z = me // 2
    x = me % 2
    relays = (zs - 1) * q

    barrier = pltpu.get_barrier_semaphore()
    for d in range(1, n):
        pl.semaphore_signal(barrier, inc=1, device_id={"client": lax.rem(me + d, n)}, device_id_type=MESH)
    for d in range(1, heads):
        pl.semaphore_signal(barrier, inc=1, device_id={"head": lax.rem(my_head + d, heads)}, device_id_type=MESH)

    after_first = (z + zs - 1) // zs
    before_last = (2 * zs - 2 - z) // zs
    middle = after_first * before_last
    upper = 2 * z // zs
    near = z + upper * (zs - 1 - 2 * z)

    def dest(k):
        both = (2 * near - k - 1 + zs) // zs
        odd = k % 2
        out = both * (odd * (k // 2) + (1 - odd) * (zs - 1 - k // 2)) + (1 - both) * (zs - 1 - k + near)
        return out + upper * (zs - 1 - 2 * out)

    def block_row(place, side):
        return (place * 2 + side) * block

    def piece_row(place, side, s):
        return pl.multiple_of(block_row(place, side) + (s + 1) * sub, sub)

    def landing(place):
        right = (place - z + zs) // zs
        target = z + 2 * right - 1
        gap = right * (place - target) + (1 - right) * (target - place)
        away = (gap + zs - 1) // zs
        slot = away * place + (1 - away) * (zs + 1 - right)
        return target * 2 + x, slot

    partner = z * 2 + 1 - x

    def unit_side(u):
        return (x + 1 - u % 2) % 2

    def unit_row(u):
        return pl.multiple_of(block_row(dest(u // 2), unit_side(u)), block)

    def pre_copy(u, h):
        columns = pl.ds(pl.multiple_of(unit_row(u) + h * piece, piece), piece)
        return pltpu.make_async_copy(
            pre_ref.at[:, columns], pre_v.at[u, :, pl.ds(pl.multiple_of(h * piece, piece), piece)],
            pre_sem.at[u * hq + h])

    chunk = math.gcd(rows, 256)
    delta_copies = [
        pltpu.make_async_copy(delta_ref.at[pl.ds(c * chunk, chunk), :], delta_v.at[pl.ds(c * chunk, chunk), :],
                              delta_sem.at[c])
        for c in range(rows // chunk)]
    weight_copy = pltpu.make_async_copy(weight_ref, weight_v, weight_sem)
    ids_copy = pltpu.make_async_copy(ids_ref, ids_all.at[me], ids_sem)
    pre_copy(0, 0).start()
    for copy in delta_copies:
        copy.start()
    ids_copy.start()
    def load(u, carry):
        @pl.when(u > 0)
        def _():
            pre_copy(u, 0).start()
        return carry
    lax.fori_loop(0, 2 * zs, load, 0)
    def load_rest(u, carry):
        for h in range(1, hq):
            pre_copy(u, h).start()
        return carry
    lax.fori_loop(0, 2 * zs, load_rest, 0)
    weight_copy.start()

    line_in[z * q] = jnp.zeros((sub, emit), BF16)
    first_in[z * 2] = jnp.zeros((sub, emit), BF16)

    step = 64
    bias = jnp.zeros((8, emit), F32)
    for c, copy in enumerate(delta_copies):
        copy.wait()
        def narrow(r, total):
            at = pl.ds(pl.multiple_of(c * chunk + r * step, step), step)
            value = delta_v[at, :]
            low[at, :] = value.astype(BF16)
            return total + jnp.sum(value.reshape(step // 8, 8, emit), axis=0)
        bias = lax.fori_loop(0, chunk // step, narrow, bias)
    bias = jnp.sum(bias, axis=0, keepdims=True)
    half = emit // 2
    pad = mine.shape[1] - spans
    tail = jnp.where(
        lax.broadcasted_iota(jnp.int32, (pad, emit), 0) == 0, jnp.broadcast_to(bias, (pad, emit)), 0.0
    ).astype(BF16)
    for h in range(2):
        mine[h, pl.ds(spans, pad), :] = tail[:, h * half:(h + 1) * half]

    pl.semaphore_wait(barrier, n - 1 + heads - 1)

    def product(u, h):
        p = pre_v[u, :, pl.ds(pl.multiple_of(h * piece, piece), piece)].astype(F32)
        hidden = (p * jax.nn.sigmoid(p)).astype(BF16)
        value = lax.dot_general(hidden, low[...], (((0,), (0,)), ((), ())), preferred_element_type=F32)
        part[pl.ds(pl.multiple_of(unit_row(u) + h * piece, piece), piece), :] = value.astype(BF16)

    def slope_sums(t):
        u = t // hq
        h = t % hq
        p = pre_v[u, :, pl.ds(pl.multiple_of(h * piece, piece), piece)].astype(F32)
        row = pl.multiple_of(unit_row(u) + h * piece, piece)
        value = lax.dot_general(
            low[...], weight_v[pl.ds(row, piece), :], (((1,), (1,)), ((), ())), preferred_element_type=F32)
        s = jax.nn.sigmoid(p)
        grad = value.astype(BF16).astype(F32) * (s * (1.0 + p * (1.0 - s)))
        grad = grad.reshape(clients, spans, piece)
        to = row // emit
        columns = pl.ds(pl.multiple_of(row % emit, piece), piece)
        small[to, pl.ds(0, spans), columns] = jnp.sum(grad, axis=0).astype(BF16)
        small[to, pl.ds(spans, clients), columns] = jnp.sum(grad, axis=1).astype(BF16)

    def pair_copy(i):
        return pltpu.make_async_remote_copy(
            src_ref=part.at[pl.ds(piece_row(dest(i // q), 1 - x, i % q), sub), :], dst_ref=pair_in.at[i],
            send_sem=pair_send.at[i], recv_sem=pair_recv.at[i],
            device_id={"client": partner}, device_id_type=MESH)

    def line_copy(i):
        place = dest(i // q)
        target, slot = landing(place)
        return pltpu.make_async_remote_copy(
            src_ref=part.at[pl.ds(piece_row(place, x, i % q), sub), :], dst_ref=line_in.at[slot * q + i % q],
            send_sem=line_send.at[i], recv_sem=line_recv.at[slot * q + i % q],
            device_id={"client": target}, device_id_type=MESH)

    def arrival(slot):
        return pltpu.make_async_remote_copy(
            src_ref=part.at[pl.ds(0, sub), :], dst_ref=line_in.at[slot], send_sem=line_send.at[0],
            recv_sem=line_recv.at[slot], device_id={"client": partner}, device_id_type=MESH)

    lead = q
    queue = 4
    slopes = 2 * zs * hq
    paced = slopes // 2 + 1
    step_rows = min(32, sub)

    def relay(i):
        place = dest(i // q)
        row = piece_row(place, x, i % q)
        pair_copy(i).wait_recv()
        @pl.when(middle == 1)
        def _():
            arrival(place * q + i % q).wait_recv()
        slot = middle * (place * q + i % q) + (1 - middle) * z * q
        def add(r, carry):
            at = pl.ds(pl.multiple_of(r * step_rows, step_rows), step_rows)
            mine_at = pl.ds(pl.multiple_of(row + r * step_rows, step_rows), step_rows)
            total = part[mine_at, :].astype(F32) + pair_in[i, at, :].astype(F32)
            part[mine_at, :] = (total + line_in[slot, at, :].astype(F32)).astype(BF16)
            return carry
        lax.fori_loop(0, sub // step_rows, add, 0)
        @pl.when(i >= paced)
        def _():
            line_copy(i - queue).wait_send()
        line_copy(i).start()
        @pl.when(i + lead < zs * q)
        def _():
            pair_copy(i + lead).start()

    def relay_range(start, stop):
        def body(i, carry):
            relay(i)
            return carry
        if stop > start:
            lax.fori_loop(start, stop, body, 0)

    def finish(s, square):
        i = relays + s
        row = piece_row(z, x, s)
        pair_copy(i).wait_recv()
        @pl.when(after_first == 1)
        def _():
            arrival(zs * q + s).wait_recv()
        @pl.when(before_last == 1)
        def _():
            arrival((zs + 1) * q + s).wait_recv()
        left = after_first * (zs * q + s) + (1 - after_first) * z * q
        right = before_last * ((zs + 1) * q + s) + (1 - before_last) * z * q
        def add(r, carry):
            at = pl.ds(pl.multiple_of(r * step_rows, step_rows), step_rows)
            mine_at = pl.ds(pl.multiple_of(row + r * step_rows, step_rows), step_rows)
            out_at = pl.ds(pl.multiple_of((s + 1) * sub + r * step_rows, step_rows), step_rows)
            total = part[mine_at, :].astype(F32) + pair_in[i, at, :].astype(F32)
            total = total + line_in[left, at, :].astype(F32) + line_in[right, at, :].astype(F32)
            head_v[out_at, :] = total
            return carry + jnp.sum((total * total).reshape(step_rows // 8, 8, emit), axis=0)
        square = lax.fori_loop(0, sub // step_rows, add, square)
        pltpu.make_async_copy(
            head_v.at[pl.ds(pl.multiple_of((s + 1) * sub, sub), sub), :],
            head_out.at[pl.ds(pl.multiple_of((s + 1) * sub, sub), sub), :], out_sem.at[s + 1]).start()
        return square

    def first_copy(j):
        place = dest(j // 2)
        side = unit_side(j)
        target, slot = landing(place)
        return pltpu.make_async_remote_copy(
            src_ref=part.at[pl.ds(pl.multiple_of(block_row(place, side), sub), sub), :],
            dst_ref=first_in.at[slot * 2 + side],
            send_sem=first_send.at[j], recv_sem=first_recv.at[slot * 2 + side],
            device_id={"client": target}, device_id_type=MESH)

    def first_arrival(slot):
        return pltpu.make_async_remote_copy(
            src_ref=part.at[pl.ds(0, sub), :], dst_ref=first_in.at[slot], send_sem=first_send.at[0],
            recv_sem=first_recv.at[slot], device_id={"client": partner}, device_id_type=MESH)

    def first_relay(j):
        @pl.when(middle == 1)
        def _():
            place = dest(j // 2)
            side = unit_side(j)
            row = pl.multiple_of(block_row(place, side), sub)
            first_arrival(place * 2 + side).wait_recv()
            def add(r, carry):
                at = pl.ds(pl.multiple_of(r * step_rows, step_rows), step_rows)
                mine_at = pl.ds(pl.multiple_of(row + r * step_rows, step_rows), step_rows)
                part[mine_at, :] = (
                    part[mine_at, :].astype(F32) + first_in[place * 2 + side, at, :].astype(F32)).astype(BF16)
                return carry
            lax.fori_loop(0, sub // step_rows, add, 0)
            first_copy(j).start()

    swap_copy = pltpu.make_async_remote_copy(
        src_ref=part.at[pl.ds(pl.multiple_of(block_row(z, 1 - x), sub), sub), :], dst_ref=swap_in,
        send_sem=swap_sem.at[0], recv_sem=swap_sem.at[1], device_id={"client": partner}, device_id_type=MESH)

    def first_wait(side):
        @pl.when(after_first == 1)
        def _():
            first_arrival(zs * 2 + side).wait_recv()
        @pl.when(before_last == 1)
        def _():
            first_arrival((zs + 1) * 2 + side).wait_recv()
        left = after_first * (zs * 2 + side) + (1 - after_first) * z * 2
        right = before_last * ((zs + 1) * 2 + side) + (1 - before_last) * z * 2
        return left, right

    def first_swap():
        row = block_row(z, 1 - x)
        left, right = first_wait(1 - x)
        def add(r, carry):
            at = pl.ds(pl.multiple_of(r * step_rows, step_rows), step_rows)
            mine_at = pl.ds(pl.multiple_of(row + r * step_rows, step_rows), step_rows)
            total = part[mine_at, :].astype(F32) + first_in[left, at, :].astype(F32)
            part[mine_at, :] = (total + first_in[right, at, :].astype(F32)).astype(BF16)
            return carry
        lax.fori_loop(0, sub // step_rows, add, 0)
        swap_copy.start()

    def first_finish(square):
        row = block_row(z, x)
        left, right = first_wait(x)
        swap_copy.wait_recv()
        def add(r, carry):
            at = pl.ds(pl.multiple_of(r * step_rows, step_rows), step_rows)
            mine_at = pl.ds(pl.multiple_of(row + r * step_rows, step_rows), step_rows)
            total = part[mine_at, :].astype(F32) + first_in[left, at, :].astype(F32)
            total = total + first_in[right, at, :].astype(F32) + swap_in[at, :].astype(F32)
            head_v[at, :] = total
            return carry + jnp.sum((total * total).reshape(step_rows // 8, 8, emit), axis=0)
        square = lax.fori_loop(0, sub // step_rows, add, square)
        pltpu.make_async_copy(head_v.at[pl.ds(0, sub), :], head_out.at[pl.ds(0, sub), :], out_sem.at[0]).start()
        return square

    ready = piece // sub - 1

    def opening(u, carry):
        pre_copy(u, 0).wait()
        product(u, 0)
        @pl.when(middle == 0)
        def _():
            first_copy(u).start()
        @pl.when(u == 0)
        def _():
            for i in range(ready):
                pair_copy(i).start()
        return carry
    lax.fori_loop(0, 2 * (zs - 1), opening, 0)
    if hq > 1:
        def second(t, carry):
            pre_copy(t // (hq - 1), 1 + t % (hq - 1)).wait()
            product(t // (hq - 1), 1 + t % (hq - 1))
            return carry
        lax.fori_loop(0, 3 * (hq - 1), second, 0)
    def more_pairs(i, carry):
        pair_copy(i).start()
        return carry
    lax.fori_loop(ready, lead, more_pairs, 0)
    first_relay(0)
    first_relay(1)
    def loaded(u, carry):
        @pl.when(u >= 2 * zs - 2)
        def _():
            pre_copy(u, 0).wait()
        for h in range(1, hq):
            pre_copy(u, h).wait()
        return carry
    lax.fori_loop(3 if hq > 1 else 2 * zs - 2, 2 * zs, loaded, 0)
    weight_copy.wait()

    ids_copy.wait()
    ids_copies = []
    for d in range(1, n):
        copy = pltpu.make_async_remote_copy(
            src_ref=ids_all.at[me], dst_ref=ids_all.at[me], send_sem=ids_send.at[d], recv_sem=ids_recv.at[me],
            device_id={"client": lax.rem(me + d, n)}, device_id_type=MESH)
        copy.start()
        ids_copies.append(copy)

    firsts = 2 * (zs - 1)
    def main(t, carry):
        slope_sums(t)
        @pl.when((t % 3 == 0) & (2 + t // 3 < firsts))
        def _():
            first_relay(2 + t // 3)
        @pl.when(t % 2 == 1)
        def _():
            relay(t // 2)
        return carry
    lax.fori_loop(0, slopes, main, 0)

    head_copies = []
    for d in range(1, heads):
        target = lax.rem(my_head + d, heads)
        copy = pltpu.make_async_remote_copy(
            src_ref=small.at[target], dst_ref=small_in.at[my_head],
            send_sem=head_send.at[d], recv_sem=head_recv.at[my_head],
            device_id={"head": target}, device_id_type=MESH)
        copy.start()
        head_copies.append(copy)

    done = 2 + (slopes + 2) // 3
    if done < firsts:
        def rest_first(j, carry):
            first_relay(j)
            return carry
        lax.fori_loop(done, firsts, rest_first, 0)

    at = slopes // 2
    if hq > 1:
        def third(t, carry):
            product(3 + t // (hq - 1), 1 + t % (hq - 1))
            return carry
        lax.fori_loop(0, (2 * zs - 5) * (hq - 1), third, 0)
    relay_range(at, at + 1)
    def fourth(t, carry):
        product(2 * zs - 2 + t // hq, t % hq)
        return carry
    lax.fori_loop(0, 2 * hq, fourth, 0)
    first_swap()
    relay_range(at + 1, at + 4)
    at = at + 4
    stop = [at + (relays - at) * k // 9 for k in (4, 8, 9)]

    for d in range(1, heads):
        source = lax.rem(my_head + d, heads)
        pltpu.make_async_remote_copy(
            src_ref=small.at[0], dst_ref=small_in.at[source], send_sem=head_send.at[d],
            recv_sem=head_recv.at[source], device_id={"head": source}, device_id_type=MESH).wait_recv()
    total = small[my_head].astype(F32)
    for d in range(1, heads):
        total = total + small_in[lax.rem(my_head + d, heads)].astype(F32)
    for h in range(2):
        mine[h, pl.ds(0, spans), :] = total[:spans, h * half:(h + 1) * half].astype(BF16)
    embed_all[z, x] = total[spans:].astype(BF16)

    embed_pair = pltpu.make_async_remote_copy(
        src_ref=embed_all.at[z, x], dst_ref=embed_all.at[z, x], send_sem=embed_pair_sem.at[0],
        recv_sem=embed_pair_sem.at[1], device_id={"client": partner}, device_id_type=MESH)
    embed_pair.start()
    roots = [zs // 2 - 1, zs // 2]
    def span_copy(h):
        return pltpu.make_async_remote_copy(
            src_ref=mine.at[h], dst_ref=span_in.at[z], send_sem=span_send.at[h], recv_sem=span_recv.at[z],
            device_id={"client": roots[h] * 2 + x}, device_id_type=MESH)
    for h in range(2):
        @pl.when(z != roots[h])
        def _():
            span_copy(h).start()

    relay_range(at, stop[0])

    embed_pair.wait_recv()
    embed_copies = []
    for d in range(1, zs):
        copy = pltpu.make_async_remote_copy(
            src_ref=embed_all.at[z], dst_ref=embed_all.at[z], send_sem=embed_send.at[d], recv_sem=embed_recv.at[z],
            device_id={"client": lax.rem(z + d, zs) * 2 + x}, device_id_type=MESH)
        copy.start()
        embed_copies.append(copy)
    span_pair_copy = pltpu.make_async_remote_copy(
        src_ref=span_part, dst_ref=span_pair, send_sem=span_pair_sem.at[0], recv_sem=span_pair_sem.at[1],
        device_id={"client": partner}, device_id_type=MESH)
    for h in range(2):
        @pl.when(z == roots[h])
        def _():
            total = mine[h].astype(F32)
            for d in range(1, zs):
                source = (roots[h] + d) % zs
                pltpu.make_async_remote_copy(
                    src_ref=mine.at[h], dst_ref=span_in.at[source], send_sem=span_send.at[h],
                    recv_sem=span_recv.at[source], device_id={"client": partner}, device_id_type=MESH).wait_recv()
                total = total + span_in[source].astype(F32)
            span_part[...] = total.astype(BF16)
            span_pair_copy.start()

    relay_range(stop[0], stop[1])

    def all_copy(h, d):
        return pltpu.make_async_remote_copy(
            src_ref=span_all.at[h], dst_ref=span_all.at[h], send_sem=all_send.at[d], recv_sem=all_recv.at[h],
            device_id={"client": lax.rem(z + d, zs) * 2 + x}, device_id_type=MESH)
    for h in range(2):
        @pl.when(z == roots[h])
        def _():
            span_pair_copy.wait_recv()
            span_all[h] = (span_part[...].astype(F32) + span_pair[...].astype(F32)).astype(BF16)
            for d in range(1, zs):
                all_copy(h, d).start()

    relay_range(stop[1], relays)
    square = jnp.zeros((8, emit), F32)
    square = first_finish(square)
    square = lax.fori_loop(0, 3, finish, square)

    for d in range(1, n):
        source = lax.rem(me + d, n)
        pltpu.make_async_remote_copy(
            src_ref=ids_all.at[me], dst_ref=ids_all.at[source], send_sem=ids_send.at[d],
            recv_sem=ids_recv.at[source], device_id={"client": source}, device_id_type=MESH).wait_recv()
    for d in range(1, zs):
        source = lax.rem(z + d, zs)
        pltpu.make_async_remote_copy(
            src_ref=embed_all.at[z], dst_ref=embed_all.at[source], send_sem=embed_send.at[d],
            recv_sem=embed_recv.at[source], device_id={"client": source * 2 + x}, device_id_type=MESH).wait_recv()
    wanted = lax.broadcasted_iota(jnp.int32, (clients, clients), 0) + me * clients
    embed_raw = jnp.zeros((clients, emit), F32)
    for c in range(n):
        chosen = (jnp.broadcast_to(ids_all[c], (clients, clients)) == wanted).astype(F32).astype(BF16)
        embed_raw = embed_raw + jnp.dot(chosen, embed_all[c // 2, c % 2], preferred_element_type=F32)
    embed_out[...] = embed_raw
    embed_square = jnp.sum(embed_raw * embed_raw)

    rest_square = jnp.zeros((), F32)
    for h in range(2):
        @pl.when(z != roots[h])
        def _():
            all_copy(h, 1).wait_recv()
        value = span_all[h].astype(F32)
        rest_out[:, pl.ds(h * half, half)] = value
        rest_square = rest_square + jnp.sum(value * value)

    square = lax.fori_loop(3, q, finish, square)
    head_total = jnp.sum(square)

    line = lax.broadcasted_iota(jnp.int32, (8, 128), 0)
    stat[0] = jnp.where(line == 0, head_total, jnp.where(line == 1, embed_square, rest_square / n))
    copies = []
    for d in range(1, n):
        copy = pltpu.make_async_remote_copy(
            src_ref=stat.at[0], dst_ref=stat_in.at[me], send_sem=stat_send.at[d - 1],
            recv_sem=stat_recv.at[me], device_id={"client": lax.rem(me + d, n)}, device_id_type=MESH)
        copy.start()
        copies.append(copy)
    stat_in[me] = stat[0]
    for d in range(1, n):
        source = lax.rem(me + d, n)
        pltpu.make_async_remote_copy(
            src_ref=stat.at[0], dst_ref=stat_in.at[source], send_sem=stat_send.at[d - 1],
            recv_sem=stat_recv.at[source], device_id={"client": source}, device_id_type=MESH).wait_recv()
    total = stat_in[0]
    for c in range(1, n):
        total = total + stat_in[c]
    stat[1] = total
    stat_head_in[my_head] = total
    more = []
    for d in range(1, heads):
        copy = pltpu.make_async_remote_copy(
            src_ref=stat.at[1], dst_ref=stat_head_in.at[my_head], send_sem=stat_send.at[n - 2 + d],
            recv_sem=stat_recv.at[n + my_head], device_id={"head": lax.rem(my_head + d, heads)}, device_id_type=MESH)
        copy.start()
        more.append(copy)
    for d in range(1, heads):
        source = lax.rem(my_head + d, heads)
        pltpu.make_async_remote_copy(
            src_ref=stat.at[1], dst_ref=stat_head_in.at[source], send_sem=stat_send.at[n - 2 + d],
            recv_sem=stat_recv.at[n + source], device_id={"head": source}, device_id_type=MESH).wait_recv()
    total = stat_head_in[0]
    for c in range(1, heads):
        total = total + stat_head_in[c]
    stat_out[...] = total

    def pair_sent(i, carry):
        pair_copy(i).wait_send()
        return carry
    lax.fori_loop(0, zs * q, pair_sent, 0)
    def line_sent(i, carry):
        line_copy(i).wait_send()
        return carry
    lax.fori_loop(0, paced - queue, line_sent, 0)
    lax.fori_loop(relays - queue, relays, line_sent, 0)
    def first_sent(j, carry):
        first_copy(j).wait_send()
        return carry
    lax.fori_loop(0, firsts, first_sent, 0)
    swap_copy.wait_send()
    embed_pair.wait_send()
    for copy in head_copies + embed_copies + ids_copies + copies + more:
        copy.wait_send()
    for h in range(2):
        @pl.when(z != roots[h])
        def _():
            span_copy(h).wait_send()
        @pl.when(z == roots[h])
        def _():
            span_pair_copy.wait_send()
            for d in range(1, zs):
                all_copy(h, d).wait_send()
    def written(s, carry):
        at = pl.multiple_of(s * sub, sub)
        pltpu.make_async_copy(
            head_v.at[pl.ds(at, sub), :], head_out.at[pl.ds(at, sub), :], out_sem.at[s]).wait()
        return carry
    lax.fori_loop(0, q + 1, written, 0)


def scale_kernel(sizes, spans, stat_ref, head_ref, rest_ref, embed_ref, head_out, bias_out, embed_out, span_out):
    head_size, embed_size, rest_size = sizes
    head_out[...] = clip_factor(stat_ref[0:1, 0:1], head_size) * head_ref[...]
    @pl.when(pl.program_id(0) == 0)
    def _():
        rest_factor = clip_factor(stat_ref[2:3, 0:1], rest_size)
        embed_out[...] = clip_factor(stat_ref[1:2, 0:1], embed_size) * embed_ref[...]
        bias_out[...] = rest_factor * rest_ref[spans:spans + 1, :]
        span_out[...] = rest_factor * rest_ref[:spans, :]


def per_device(n, heads, pre, delta, head_weight, client_ids):
    rows, hidden_width = pre.shape
    emit = delta.shape[1]
    clients = client_ids.shape[0]
    spans = rows // clients
    block = hidden_width // n
    piece = min(256, block)
    hq = block // piece
    zs = n // 2
    q = 7
    sub = block // (q + 1)
    padded = (spans + 16) // 16 * 16
    half = emit // 2
    cfg = (n, heads, block, piece, spans, clients)
    ids = client_ids.reshape(1, clients)
    hbm = pl.BlockSpec(memory_space=pl.ANY)
    vmem = pl.BlockSpec(memory_space=pltpu.VMEM)
    dma = pltpu.SemaphoreType.DMA
    chunk = math.gcd(rows, 256)
    head_raw, rest_raw, embed_raw, stats = pl.pallas_call(
        functools.partial(kernel, cfg),
        out_shape=(
            jax.ShapeDtypeStruct((block, emit), F32),
            jax.ShapeDtypeStruct((padded, emit), F32),
            jax.ShapeDtypeStruct((clients, emit), F32),
            jax.ShapeDtypeStruct((8, 128), F32),
        ),
        in_specs=[hbm, hbm, hbm, hbm],
        out_specs=(hbm, vmem, vmem, vmem),
        scratch_shapes=[
            pltpu.VMEM((n, rows, block), BF16),
            pltpu.VMEM((rows, emit), F32),
            pltpu.VMEM((rows, emit), BF16),
            pltpu.VMEM((hidden_width, emit), BF16),
            pltpu.VMEM((hidden_width, emit), BF16),
            pltpu.VMEM((zs * q, sub, emit), BF16),
            pltpu.VMEM(((zs + 2) * q, sub, emit), BF16),
            pltpu.VMEM(((zs + 2) * 2, sub, emit), BF16),
            pltpu.VMEM((sub, emit), BF16),
            pltpu.VMEM((block, emit), F32),
            pltpu.VMEM((heads, spans + clients, emit), BF16),
            pltpu.VMEM((heads, spans + clients, emit), BF16),
            pltpu.VMEM((2, padded, half), BF16),
            pltpu.VMEM((zs, padded, half), BF16),
            pltpu.VMEM((padded, half), BF16),
            pltpu.VMEM((padded, half), BF16),
            pltpu.VMEM((2, padded, half), BF16),
            pltpu.VMEM((zs, 2, clients, emit), BF16),
            pltpu.VMEM((n, 1, clients), jnp.int32),
            pltpu.VMEM((2, 8, 128), F32),
            pltpu.VMEM((n, 8, 128), F32),
            pltpu.VMEM((heads, 8, 128), F32),
            dma((n * hq,)), dma((rows // chunk,)), dma, dma((q + 1,)),
            dma((zs * q,)), dma((zs * q,)), dma(((zs - 1) * q,)), dma(((zs + 2) * q,)),
            dma((2 * (zs - 1),)), dma(((zs + 2) * 2,)), dma((2,)), dma((heads,)), dma((heads,)),
            dma((2,)), dma((zs,)), dma((2,)), dma((zs,)), dma((2,)), dma((2,)), dma((zs,)), dma((zs,)),
            dma, dma((n,)), dma((n,)), dma((n + heads - 2,)), dma((n + heads,)),
        ],
        compiler_params=pltpu.CompilerParams(
            collective_id=0, has_side_effects=True, vmem_limit_bytes=62 * 2**20
        ),
        name="clipped_grads",
    )(pre, delta, head_weight, ids)
    sizes = (hidden_width * emit * heads, clients * n * hidden_width, spans * hidden_width + emit * heads)
    steps = 4 if block % 32 == 0 else 1
    whole = lambda *shape: pl.BlockSpec(shape, lambda i: (0, 0))
    tile = pl.BlockSpec((block // steps, emit), lambda i: (i, 0))
    head_grad, bias_grad, embed_grad, span_grad = pl.pallas_call(
        functools.partial(scale_kernel, sizes, spans),
        grid=(steps,),
        out_shape=(
            jax.ShapeDtypeStruct((block, emit), F32),
            jax.ShapeDtypeStruct((1, emit), F32),
            jax.ShapeDtypeStruct((clients, emit), F32),
            jax.ShapeDtypeStruct((spans, emit), F32),
        ),
        in_specs=[whole(8, 128), tile, whole(padded, emit), whole(clients, emit)],
        out_specs=(tile, whole(1, emit), whole(clients, emit), whole(spans, emit)),
        name="scaled",
    )(stats, head_raw, rest_raw, embed_raw)
    return head_grad, bias_grad.reshape(emit), embed_grad, span_grad


def solution(mesh):
    placed = (P("client", None), P("client", "head"), P(None, "head"), P("client"))
    return jax.shard_map(
        functools.partial(per_device, mesh.shape["client"], mesh.shape["head"]),
        mesh=mesh,
        in_specs=placed,
        out_specs=(P("client", "head"), P("head"), P("client", "head"), P(None, "head")),
        check_vma=False,
    )
```

time: 149 us -> 110 us (0.74)
  Pallas kernels: 135 us -> 110 us
  other arithmetic: 7.76 us -> 0 us
  local copies, waits for them, and re-layouts: 2.62 us -> 0 us
  between operations: 2.72 us -> 0.64 us
    pallas_call x1, Pallas kernels: 135 us -> 105 us  [per_device(): pl.pallas_call(functools.partial(kernel, cfg), out_shape=(jax.ShapeDtypeS...]
    mul x4 -> x0, other arithmetic: 7.76 us -> none  [the longest x1 3.2 us: per_device(): head_factor * head_raw]
    pallas_call x0 -> x1, Pallas kernels: none -> 4.23 us  [per_device(): pl.pallas_call(functools.partial(scale_kernel, sizes, spans), grid=(steps...]
where the time goes in v1:
time: 110 us
  Pallas kernels  110 us (100%)
    pallas_call x1, Pallas kernels, per_device(): pl.pallas_call(functools.partial(kernel, cfg), out_shape=(jax.ShapeDtypeS...  105 us
    pallas_call x1, Pallas kernels, per_device(): pl.pallas_call(functools.partial(scale_kernel, sizes, spans), grid=(steps...  4.23 us

profile of v1, /device:TPU:0, one launch (start us, length us, event | category | flops | bytes accessed | tf_op | source)
XLA Modules:
  0.0 110.3 jit_solution(15042487261234264832)
XLA Ops:
  0.6 105.4 %clipped_grads.1 = (f32[512,1024]{1,0:T(8,128)}, f32[96,1024]{1,0:T(8,128)}, f32[16,1024]{1,0:T(8,128)}, f32[8,128]{1,0:T(8,128)}) custom-call(bf16[1280,4096]{1,0:T(8,128)(2,1)} %pre_ref.1, f32[1280,1024]{1,0:T(8,128)} %delta_ref.1, bf16[4096,1024]{1,0:T(8,128)(2,1)} %weight_ref.1, s32[1,16]{1,0:T(1,128)} %bitcast.2), custom_call_target="tpu_custom_call" | custom-call | tf_op jit(solution)/shard_map/clipped_grads/pallas_call | solution.py:602
  106.1 4.2 %scaled.1 = (f32[512,1024]{1,0:T(8,128)}, f32[1,1024]{1,0:T(1,128)}, f32[16,1024]{1,0:T(8,128)}, f32[80,1024]{1,0:T(8,128)}) custom-call(f32[8,128]{1,0:T(8,128)} %get-tuple-element.12.stat_ref, f32[512,1024]{1,0:T(8,128)} %get-tuple-element.13.head_ref, f32[96,1024]{1,0:T(8,128)} %get-tuple-element.14.rest_ref, f32[16,1024]{1,0:T(8,128)} %get-tuple-element.15.embed_ref), custom_call_target="tpu_custom_call" | custom-call | tf_op jit(solution)/shard_map/scaled/pallas_call | solution.py:650

commit v2 on v1

--- a/solution.py
+++ b/solution.py
@@ -21,10 +21,10 @@
 def kernel(cfg, pre_ref, delta_ref, weight_ref, ids_ref, head_out, rest_out, embed_out, stat_out,
            pre_v, delta_v, low, weight_v, part, pair_in, line_in, first_in, swap_in, head_v,
            small, small_in, mine, span_in, span_part, span_pair, span_all, embed_all, ids_all,
-           stat, stat_in, stat_head_in,
+           embed_v, rest_v, stat_all,
            pre_sem, delta_sem, weight_sem, out_sem, pair_send, pair_recv, line_send, line_recv,
            first_send, first_recv, swap_sem, head_send, head_recv, span_send, span_recv, span_pair_sem,
-           all_send, all_recv, embed_pair_sem, embed_send, embed_recv, ids_sem, ids_send, ids_recv,
+           all_send, all_recv, write_sem, embed_pair_sem, embed_send, embed_recv, ids_sem, ids_send, ids_recv,
            stat_send, stat_recv):
     n, heads, block, piece, spans, clients = cfg
     zs = n // 2
@@ -38,11 +38,18 @@
     x = me % 2
     relays = (zs - 1) * q
 
+    devices = n * heads
+    flat = me * heads + my_head
+
+    def device(d):
+        other = lax.rem(flat + d, devices)
+        return {"client": other // heads, "head": other % heads}
+
     barrier = pltpu.get_barrier_semaphore()
-    for d in range(1, n):
-        pl.semaphore_signal(barrier, inc=1, device_id={"client": lax.rem(me + d, n)}, device_id_type=MESH)
-    for d in range(1, heads):
-        pl.semaphore_signal(barrier, inc=1, device_id={"head": lax.rem(my_head + d, heads)}, device_id_type=MESH)
+    def greet(d, carry):
+        pl.semaphore_signal(barrier, inc=1, device_id=device(d), device_id_type=MESH)
+        return carry
+    lax.fori_loop(1, devices, greet, 0)
 
     after_first = (z + zs - 1) // zs
     before_last = (2 * zs - 2 - z) // zs
@@ -112,25 +119,15 @@
     first_in[z * 2] = jnp.zeros((sub, emit), BF16)
 
     step = 64
-    bias = jnp.zeros((8, emit), F32)
     for c, copy in enumerate(delta_copies):
         copy.wait()
-        def narrow(r, total):
+        def narrow(r, carry):
             at = pl.ds(pl.multiple_of(c * chunk + r * step, step), step)
-            value = delta_v[at, :]
-            low[at, :] = value.astype(BF16)
-            return total + jnp.sum(value.reshape(step // 8, 8, emit), axis=0)
-        bias = lax.fori_loop(0, chunk // step, narrow, bias)
-    bias = jnp.sum(bias, axis=0, keepdims=True)
-    half = emit // 2
-    pad = mine.shape[1] - spans
-    tail = jnp.where(
-        lax.broadcasted_iota(jnp.int32, (pad, emit), 0) == 0, jnp.broadcast_to(bias, (pad, emit)), 0.0
-    ).astype(BF16)
-    for h in range(2):
-        mine[h, pl.ds(spans, pad), :] = tail[:, h * half:(h + 1) * half]
-
-    pl.semaphore_wait(barrier, n - 1 + heads - 1)
+            low[at, :] = delta_v[at, :].astype(BF16)
+            return carry
+        lax.fori_loop(0, chunk // step, narrow, 0)
+
+    pl.semaphore_wait(barrier, devices - 1)
 
     def product(u, h):
         p = pre_v[u, :, pl.ds(pl.multiple_of(h * piece, piece), piece)].astype(F32)
@@ -172,7 +169,7 @@
             src_ref=part.at[pl.ds(0, sub), :], dst_ref=line_in.at[slot], send_sem=line_send.at[0],
             recv_sem=line_recv.at[slot], device_id={"client": partner}, device_id_type=MESH)
 
-    lead = q
+    lead = q + 2
     queue = 4
     slopes = 2 * zs * hq
     paced = slopes // 2 + 1
@@ -381,6 +378,19 @@
             return carry
         lax.fori_loop(done, firsts, rest_first, 0)
 
+    def add_rows(r, total):
+        value = delta_v[pl.ds(pl.multiple_of(r * step, step), step), :]
+        return total + jnp.sum(value.reshape(step // 8, 8, emit), axis=0)
+    bias = lax.fori_loop(0, rows // step, add_rows, jnp.zeros((8, emit), F32))
+    bias = jnp.sum(bias, axis=0, keepdims=True)
+    half = emit // 2
+    pad = mine.shape[1] - spans
+    tail = jnp.where(
+        lax.broadcasted_iota(jnp.int32, (pad, emit), 0) == 0, jnp.broadcast_to(bias, (pad, emit)), 0.0
+    ).astype(BF16)
+    for h in range(2):
+        mine[h, pl.ds(spans, pad), :] = tail[:, h * half:(h + 1) * half]
+
     at = slopes // 2
     if hq > 1:
         def third(t, carry):
@@ -483,7 +493,9 @@
     for c in range(n):
         chosen = (jnp.broadcast_to(ids_all[c], (clients, clients)) == wanted).astype(F32).astype(BF16)
         embed_raw = embed_raw + jnp.dot(chosen, embed_all[c // 2, c % 2], preferred_element_type=F32)
-    embed_out[...] = embed_raw
+    embed_v[...] = embed_raw
+    embed_write = pltpu.make_async_copy(embed_v, embed_out, write_sem.at[0])
+    embed_write.start()
     embed_square = jnp.sum(embed_raw * embed_raw)
 
     rest_square = jnp.zeros((), F32)
@@ -492,49 +504,38 @@
         def _():
             all_copy(h, 1).wait_recv()
         value = span_all[h].astype(F32)
-        rest_out[:, pl.ds(h * half, half)] = value
+        rest_v[:, pl.ds(h * half, half)] = value
         rest_square = rest_square + jnp.sum(value * value)
+
+    rest_write = pltpu.make_async_copy(rest_v, rest_out, write_sem.at[1])
+    rest_write.start()
 
     square = lax.fori_loop(3, q, finish, square)
     head_total = jnp.sum(square)
 
-    line = lax.broadcasted_iota(jnp.int32, (8, 128), 0)
-    stat[0] = jnp.where(line == 0, head_total, jnp.where(line == 1, embed_square, rest_square / n))
-    copies = []
-    for d in range(1, n):
-        copy = pltpu.make_async_remote_copy(
-            src_ref=stat.at[0], dst_ref=stat_in.at[me], send_sem=stat_send.at[d - 1],
-            recv_sem=stat_recv.at[me], device_id={"client": lax.rem(me + d, n)}, device_id_type=MESH)
-        copy.start()
-        copies.append(copy)
-    stat_in[me] = stat[0]
-    for d in range(1, n):
-        source = lax.rem(me + d, n)
+    lane = lax.broadcasted_iota(jnp.int32, (1, 128), 1)
+    stat_all[flat] = jnp.where(lane == 0, head_total, jnp.where(lane == 1, embed_square, rest_square / n))
+    def stat_copy(d):
+        return pltpu.make_async_remote_copy(
+            src_ref=stat_all.at[flat], dst_ref=stat_all.at[flat], send_sem=stat_send.at[d],
+            recv_sem=stat_recv.at[flat], device_id=device(d), device_id_type=MESH)
+    def tell(d, carry):
+        stat_copy(d).start()
+        return carry
+    lax.fori_loop(1, devices, tell, 0)
+    def hear(d, carry):
+        source = lax.rem(flat + d, devices)
         pltpu.make_async_remote_copy(
-            src_ref=stat.at[0], dst_ref=stat_in.at[source], send_sem=stat_send.at[d - 1],
-            recv_sem=stat_recv.at[source], device_id={"client": source}, device_id_type=MESH).wait_recv()
-    total = stat_in[0]
-    for c in range(1, n):
-        total = total + stat_in[c]
-    stat[1] = total
-    stat_head_in[my_head] = total
-    more = []
-    for d in range(1, heads):
-        copy = pltpu.make_async_remote_copy(
-            src_ref=stat.at[1], dst_ref=stat_head_in.at[my_head], send_sem=stat_send.at[n - 2 + d],
-            recv_sem=stat_recv.at[n + my_head], device_id={"head": lax.rem(my_head + d, heads)}, device_id_type=MESH)
-        copy.start()
-        more.append(copy)
-    for d in range(1, heads):
-        source = lax.rem(my_head + d, heads)
-        pltpu.make_async_remote_copy(
-            src_ref=stat.at[1], dst_ref=stat_head_in.at[source], send_sem=stat_send.at[n - 2 + d],
-            recv_sem=stat_recv.at[n + source], device_id={"head": source}, device_id_type=MESH).wait_recv()
-    total = stat_head_in[0]
-    for c in range(1, heads):
-        total = total + stat_head_in[c]
-    stat_out[...] = total
-
+            src_ref=stat_all.at[flat], dst_ref=stat_all.at[source], send_sem=stat_send.at[d],
+            recv_sem=stat_recv.at[source], device_id=device(d), device_id_type=MESH).wait_recv()
+        return carry
+    lax.fori_loop(1, devices, hear, 0)
+    stat_out[...] = jnp.sum(stat_all[...], axis=0)
+
+    def told(d, carry):
+        stat_copy(d).wait_send()
+        return carry
+    lax.fori_loop(1, devices, told, 0)
     def pair_sent(i, carry):
         pair_copy(i).wait_send()
         return carry
@@ -550,7 +551,9 @@
     lax.fori_loop(0, firsts, first_sent, 0)
     swap_copy.wait_send()
     embed_pair.wait_send()
-    for copy in head_copies + embed_copies + ids_copies + copies + more:
+    embed_write.wait()
+    rest_write.wait()
+    for copy in head_copies + embed_copies + ids_copies:
         copy.wait_send()
     for h in range(2):
         @pl.when(z != roots[h])
@@ -569,15 +572,44 @@
     lax.fori_loop(0, q + 1, written, 0)
 
 
-def scale_kernel(sizes, spans, stat_ref, head_ref, rest_ref, embed_ref, head_out, bias_out, embed_out, span_out):
+def scale_kernel(sizes, stat_ref, head_ref, rest_ref, embed_ref, head_out, bias_out, embed_out, span_out,
+                 stat, head, rest, embed, in_sem, out_sem):
     head_size, embed_size, rest_size = sizes
-    head_out[...] = clip_factor(stat_ref[0:1, 0:1], head_size) * head_ref[...]
-    @pl.when(pl.program_id(0) == 0)
-    def _():
-        rest_factor = clip_factor(stat_ref[2:3, 0:1], rest_size)
-        embed_out[...] = clip_factor(stat_ref[1:2, 0:1], embed_size) * embed_ref[...]
-        bias_out[...] = rest_factor * rest_ref[spans:spans + 1, :]
-        span_out[...] = rest_factor * rest_ref[:spans, :]
+    spans = span_out.shape[0]
+    steps = in_sem.shape[0] - 3
+    rows = head.shape[0] // steps
+    stat_in = pltpu.make_async_copy(stat_ref, stat, in_sem.at[steps])
+    rest_in = pltpu.make_async_copy(rest_ref, rest, in_sem.at[steps + 1])
+    embed_in = pltpu.make_async_copy(embed_ref, embed, in_sem.at[steps + 2])
+    def part(ref, i):
+        return ref.at[pl.ds(i * rows, rows), :]
+    stat_in.start()
+    heads_in = [pltpu.make_async_copy(part(head_ref, i), part(head, i), in_sem.at[i]) for i in range(steps)]
+    heads_out = [pltpu.make_async_copy(part(head, i), part(head_out, i), out_sem.at[i]) for i in range(steps)]
+    for copy in heads_in:
+        copy.start()
+    rest_in.start()
+    embed_in.start()
+    stat_in.wait()
+    factor = clip_factor(stat[0:1, 0:1], head_size)
+    embed_factor = clip_factor(stat[0:1, 1:2], embed_size)
+    rest_factor = clip_factor(stat[0:1, 2:3], rest_size)
+    for i in range(steps):
+        heads_in[i].wait()
+        head[pl.ds(i * rows, rows), :] = factor * head[pl.ds(i * rows, rows), :]
+        heads_out[i].start()
+    rest_in.wait()
+    rest[...] = rest_factor * rest[...]
+    bias_copy = pltpu.make_async_copy(rest.at[pl.ds(spans, 1), :], bias_out, out_sem.at[steps])
+    span_copy = pltpu.make_async_copy(rest.at[pl.ds(0, spans), :], span_out, out_sem.at[steps + 1])
+    bias_copy.start()
+    span_copy.start()
+    embed_in.wait()
+    embed[...] = embed_factor * embed[...]
+    embed_copy = pltpu.make_async_copy(embed, embed_out, out_sem.at[steps + 2])
+    embed_copy.start()
+    for copy in heads_out + [bias_copy, span_copy, embed_copy]:
+        copy.wait()
 
 
 def per_device(n, heads, pre, delta, head_weight, client_ids):
@@ -605,10 +637,10 @@
             jax.ShapeDtypeStruct((block, emit), F32),
             jax.ShapeDtypeStruct((padded, emit), F32),
             jax.ShapeDtypeStruct((clients, emit), F32),
-            jax.ShapeDtypeStruct((8, 128), F32),
+            jax.ShapeDtypeStruct((1, 128), F32),
         ),
         in_specs=[hbm, hbm, hbm, hbm],
-        out_specs=(hbm, vmem, vmem, vmem),
+        out_specs=(hbm, hbm, hbm, vmem),
         scratch_shapes=[
             pltpu.VMEM((n, rows, block), BF16),
             pltpu.VMEM((rows, emit), F32),
@@ -629,14 +661,14 @@
             pltpu.VMEM((2, padded, half), BF16),
             pltpu.VMEM((zs, 2, clients, emit), BF16),
             pltpu.VMEM((n, 1, clients), jnp.int32),
-            pltpu.VMEM((2, 8, 128), F32),
-            pltpu.VMEM((n, 8, 128), F32),
-            pltpu.VMEM((heads, 8, 128), F32),
+            pltpu.VMEM((clients, emit), F32),
+            pltpu.VMEM((padded, emit), F32),
+            pltpu.VMEM((n * heads, 1, 128), F32),
             dma((n * hq,)), dma((rows // chunk,)), dma, dma((q + 1,)),
             dma((zs * q,)), dma((zs * q,)), dma(((zs - 1) * q,)), dma(((zs + 2) * q,)),
             dma((2 * (zs - 1),)), dma(((zs + 2) * 2,)), dma((2,)), dma((heads,)), dma((heads,)),
-            dma((2,)), dma((zs,)), dma((2,)), dma((zs,)), dma((2,)), dma((2,)), dma((zs,)), dma((zs,)),
-            dma, dma((n,)), dma((n,)), dma((n + heads - 2,)), dma((n + heads,)),
+            dma((2,)), dma((zs,)), dma((2,)), dma((zs,)), dma((2,)), dma((2,)), dma((2,)), dma((zs,)), dma((zs,)),
+            dma, dma((n,)), dma((n,)), dma((n * heads,)), dma((n * heads,)),
         ],
         compiler_params=pltpu.CompilerParams(
             collective_id=0, has_side_effects=True, vmem_limit_bytes=62 * 2**20
@@ -644,20 +676,24 @@
         name="clipped_grads",
     )(pre, delta, head_weight, ids)
     sizes = (hidden_width * emit * heads, clients * n * hidden_width, spans * hidden_width + emit * heads)
-    steps = 4 if block % 32 == 0 else 1
-    whole = lambda *shape: pl.BlockSpec(shape, lambda i: (0, 0))
-    tile = pl.BlockSpec((block // steps, emit), lambda i: (i, 0))
+    steps = 4
     head_grad, bias_grad, embed_grad, span_grad = pl.pallas_call(
-        functools.partial(scale_kernel, sizes, spans),
-        grid=(steps,),
+        functools.partial(scale_kernel, sizes),
         out_shape=(
             jax.ShapeDtypeStruct((block, emit), F32),
             jax.ShapeDtypeStruct((1, emit), F32),
             jax.ShapeDtypeStruct((clients, emit), F32),
             jax.ShapeDtypeStruct((spans, emit), F32),
         ),
-        in_specs=[whole(8, 128), tile, whole(padded, emit), whole(clients, emit)],
-        out_specs=(tile, whole(1, emit), whole(clients, emit), whole(spans, emit)),
+        in_specs=[hbm] * 4,
+        out_specs=(hbm,) * 4,
+        scratch_shapes=[
+            pltpu.VMEM((1, 128), F32),
+            pltpu.VMEM((block, emit), F32),
+            pltpu.VMEM((padded, emit), F32),
+            pltpu.VMEM((clients, emit), F32),
+            dma((steps + 3,)), dma((steps + 3,)),
+        ],
         name="scaled",
     )(stats, head_raw, rest_raw, embed_raw)
     return head_grad, bias_grad.reshape(emit), embed_grad, span_grad

time: 110 us -> 109 us (level)
  Pallas kernels: 110 us -> 108 us
    pallas_call x1, Pallas kernels: 4.23 us -> 2.7 us  [per_device(): pl.pallas_call(functools.partial(scale_kernel, sizes), out_shape=(jax.Sha...]
where the time goes in v2:
time: 109 us
  Pallas kernels  108 us (99%)
    pallas_call x1, Pallas kernels, per_device(): pl.pallas_call(functools.partial(kernel, cfg), out_shape=(jax.ShapeDtypeS...  105 us
    pallas_call x1, Pallas kernels, per_device(): pl.pallas_call(functools.partial(scale_kernel, sizes), out_shape=(jax.Sha...  2.7 us

profile of v2, /device:TPU:0, one launch (start us, length us, event | category | flops | bytes accessed | tf_op | source)
XLA Modules:
  0.0 108.6 jit_solution(1542431091713959137)
XLA Ops:
  0.6 105.3 %clipped_grads.1 = (f32[512,1024]{1,0:T(8,128)}, f32[96,1024]{1,0:T(8,128)}, f32[16,1024]{1,0:T(8,128)}, f32[1,128]{1,0:T(1,128)}) custom-call(bf16[1280,4096]{1,0:T(8,128)(2,1)} %pre_ref.1, f32[1280,1024]{1,0:T(8,128)} %delta_ref.1, bf16[4096,1024]{1,0:T(8,128)(2,1)} %weight_ref.1, s32[1,16]{1,0:T(1,128)} %bitcast.2), custom_call_target="tpu_custom_call" | custom-call | tf_op jit(solution)/shard_map/clipped_grads/pallas_call | solution.py:634
  105.9 2.7 %scaled.1 = (f32[512,1024]{1,0:T(8,128)}, f32[1,1024]{1,0:T(1,128)}, f32[16,1024]{1,0:T(8,128)}, f32[80,1024]{1,0:T(8,128)}) custom-call(f32[1,128]{1,0:T(1,128)} %get-tuple-element.12.stat_ref, f32[512,1024]{1,0:T(8,128)} %get-tuple-element.13.head_ref, f32[96,1024]{1,0:T(8,128)} %get-tuple-element.14.rest_ref, f32[16,1024]{1,0:T(8,128)} %get-tuple-element.15.embed_ref), custom_call_target="tpu_custom_call" | custom-call | tf_op jit(solution)/shard_map/scaled/pallas_call | solution.py:680

commit v3 on v2

v3 whole, which is shorter than its diff:
```python
import functools
import math

import jax
import jax.numpy as jnp
from jax import lax
from jax.experimental import pallas as pl
from jax.experimental.pallas import tpu as pltpu
from jax.sharding import PartitionSpec as P

EPSILON = 1e-06
MESH = pl.DeviceIdType.MESH
F32 = jnp.float32
BF16 = jnp.bfloat16


def clip_factor(total, number):
    return jnp.minimum(1.0, 1.0 / jnp.sqrt(total / number + EPSILON))


def kernel(cfg, pre_ref, delta_ref, weight_ref, ids_ref, head_out, rest_out, embed_out, stat_out,
           pre_v, delta_v, low, weight_v, part, pair_in, line_in, first_in, swap_in, head_v,
           small, small_in, mine, span_in, span_part, span_pair, span_all, embed_all, ids_all,
           embed_v, rest_v, stat_all,
           pre_sem, delta_sem, weight_sem, out_sem, pair_send, pair_recv, line_send, line_recv,
           first_send, first_recv, swap_sem, head_send, head_recv, span_send, span_recv, span_pair_sem,
           all_send, all_recv, write_sem, embed_pair_sem, embed_send, embed_recv, ids_sem, ids_send, ids_recv,
           stat_send, stat_recv):
    n, heads, block, piece, spans, clients = cfg
    zs = n // 2
    q = 7
    sub = block // (q + 1)
    hq = block // piece
    rows, emit = low.shape
    half = emit // 2
    me = lax.axis_index("client")
    my_head = lax.axis_index("head")
    z = me // 2
    x = me % 2
    relays = (zs - 1) * q
    firsts = 2 * (zs - 1)
    slopes = 2 * zs * hq
    devices = n * heads
    flat = me * heads + my_head

    after_first = (z + zs - 1) // zs
    before_last = (2 * zs - 2 - z) // zs
    middle = after_first * before_last
    upper = 2 * z // zs
    near = z + upper * (zs - 1 - 2 * z)
    partner = z * 2 + 1 - x

    def wait_all(ref, sem):
        pltpu.make_async_copy(ref, ref, sem).wait()

    def send(src, dst, send_sem, recv_sem, client):
        return pltpu.make_async_remote_copy(
            src_ref=src, dst_ref=dst, send_sem=send_sem, recv_sem=recv_sem,
            device_id={"client": client}, device_id_type=MESH)

    def dest(k):
        both = (2 * near - k - 1 + zs) // zs
        odd = k % 2
        out = both * (odd * (k // 2) + (1 - odd) * (zs - 1 - k // 2)) + (1 - both) * (zs - 1 - k + near)
        return out + upper * (zs - 1 - 2 * out)

    def block_row(place, side):
        return (place * 2 + side) * block

    def piece_row(place, side, s):
        return pl.multiple_of(block_row(place, side) + (s + 1) * sub, sub)

    def landing(place):
        right = (place - z + zs) // zs
        target = z + 2 * right - 1
        gap = right * (place - target) + (1 - right) * (target - place)
        away = (gap + zs - 1) // zs
        slot = away * place + (1 - away) * (zs + 1 - right)
        sem = away * place + (1 - away) * (right * zs + (1 - right) * place)
        return target * 2 + x, slot, sem

    def unit_side(u):
        return (x + 1 - u % 2) % 2

    def unit_row(u):
        return pl.multiple_of(block_row(dest(u // 2), unit_side(u)), block)

    def pre_copy(u, h, sem):
        columns = pl.ds(pl.multiple_of(unit_row(u) + h * piece, piece), piece)
        return pltpu.make_async_copy(
            pre_ref.at[:, columns], pre_v.at[u, :, pl.ds(pl.multiple_of(h * piece, piece), piece)], pre_sem.at[sem])

    chunk = math.gcd(rows, 256)
    delta_copies = [
        pltpu.make_async_copy(delta_ref.at[pl.ds(c * chunk, chunk), :], delta_v.at[pl.ds(c * chunk, chunk), :],
                              delta_sem.at[c])
        for c in range(rows // chunk)]
    weight_copy = pltpu.make_async_copy(weight_ref, weight_v, weight_sem)
    ids_copy = pltpu.make_async_copy(ids_ref, ids_all.at[me], ids_sem)
    pre_copy(0, 0, 0).start()
    for copy in delta_copies:
        copy.start()

    def device(d):
        other = lax.rem(flat + d, devices)
        return {"client": other // heads, "head": other % heads}

    barrier = pltpu.get_barrier_semaphore()
    def greet(d, carry):
        pl.semaphore_signal(barrier, inc=1, device_id=device(d), device_id_type=MESH)
        return carry
    lax.fori_loop(1, devices, greet, 0)

    def load(u, carry):
        pre_copy(u, 0, 1).start()
        return carry
    lax.fori_loop(1, firsts, load, 0)
    def load_rest(u, carry):
        @pl.when(u >= firsts)
        def _():
            pre_copy(u, 0, 2).start()
        for h in range(1, hq):
            pre_copy(u, h, 2).start()
        return carry
    lax.fori_loop(0 if hq > 1 else firsts, 2 * zs, load_rest, 0)
    weight_copy.start()
    ids_copy.start()

    def product(u, h):
        p = pre_v[u, :, pl.ds(pl.multiple_of(h * piece, piece), piece)].astype(F32)
        hidden = (p * jax.nn.sigmoid(p)).astype(BF16)
        value = lax.dot_general(hidden, low[...], (((0,), (0,)), ((), ())), preferred_element_type=F32)
        part[pl.ds(pl.multiple_of(unit_row(u) + h * piece, piece), piece), :] = value.astype(BF16)

    def slope_sums(t):
        u = t // hq
        h = t % hq
        p = pre_v[u, :, pl.ds(pl.multiple_of(h * piece, piece), piece)].astype(F32)
        row = pl.multiple_of(unit_row(u) + h * piece, piece)
        value = lax.dot_general(
            low[...], weight_v[pl.ds(row, piece), :], (((1,), (1,)), ((), ())), preferred_element_type=F32)
        s = jax.nn.sigmoid(p)
        grad = value.astype(BF16).astype(F32) * (s * (1.0 + p * (1.0 - s)))
        grad = grad.reshape(clients, spans, piece)
        to = row // emit
        columns = pl.ds(pl.multiple_of(row % emit, piece), piece)
        small[to, pl.ds(0, spans), columns] = jnp.sum(grad, axis=0).astype(BF16)
        small[to, pl.ds(spans, clients), columns] = jnp.sum(grad, axis=1).astype(BF16)

    def pair_copy(i):
        return send(part.at[pl.ds(piece_row(dest(i // q), 1 - x, i % q), sub), :], pair_in.at[i],
                    pair_send, pair_recv.at[i], partner)

    queue = 3

    def line_copy(i):
        place = dest(i // q)
        target, slot, sem = landing(place)
        return send(part.at[pl.ds(piece_row(place, x, i % q), sub), :], line_in.at[slot * q + i % q],
                    line_send.at[i % queue], line_recv.at[sem * q + i % q], target)

    lead = q + 4 * middle
    step_rows = min(32, sub)

    def relay(i):
        place = dest(i // q)
        row = piece_row(place, x, i % q)
        pair_copy(i).wait_recv()
        @pl.when(middle == 1)
        def _():
            wait_all(line_in.at[place * q + i % q], line_recv.at[place * q + i % q])
        slot = middle * (place * q + i % q) + (1 - middle) * z * q
        def add(r, carry):
            at = pl.ds(pl.multiple_of(r * step_rows, step_rows), step_rows)
            mine_at = pl.ds(pl.multiple_of(row + r * step_rows, step_rows), step_rows)
            total = part[mine_at, :].astype(F32) + pair_in[i, at, :].astype(F32)
            part[mine_at, :] = (total + line_in[slot, at, :].astype(F32)).astype(BF16)
            return carry
        lax.fori_loop(0, sub // step_rows, add, 0)
        @pl.when(i >= queue)
        def _():
            line_copy(i - queue).wait_send()
        line_copy(i).start()
        @pl.when(i + lead < zs * q)
        def _():
            pair_copy(i + lead).start()

    def relay_range(start, stop):
        def body(i, carry):
            relay(i)
            return carry
        lax.fori_loop(start, stop, body, 0)

    def finish(s, square):
        i = relays + s
        row = piece_row(z, x, s)
        pair_copy(i).wait_recv()
        @pl.when(after_first == 1)
        def _():
            wait_all(line_in.at[zs * q + s], line_recv.at[zs * q + s])
        @pl.when(before_last == 1)
        def _():
            wait_all(line_in.at[(zs + 1) * q + s], line_recv.at[z * q + s])
        left = after_first * (zs * q + s) + (1 - after_first) * z * q
        right = before_last * ((zs + 1) * q + s) + (1 - before_last) * z * q
        def add(r, carry):
            at = pl.ds(pl.multiple_of(r * step_rows, step_rows), step_rows)
            mine_at = pl.ds(pl.multiple_of(row + r * step_rows, step_rows), step_rows)
            out_at = pl.ds(pl.multiple_of((s + 1) * sub + r * step_rows, step_rows), step_rows)
            total = part[mine_at, :].astype(F32) + pair_in[i, at, :].astype(F32)
            total = total + line_in[left, at, :].astype(F32) + line_in[right, at, :].astype(F32)
            head_v[out_at, :] = total
            return carry + jnp.sum((total * total).reshape(step_rows // 8, 8, emit), axis=0)
        square = lax.fori_loop(0, sub // step_rows, add, square)
        at = pl.ds(pl.multiple_of((s + 1) * sub, sub), sub)
        pltpu.make_async_copy(head_v.at[at, :], head_out.at[at, :], out_sem).start()
        return square

    def first_copy(j):
        place = dest(j // 2)
        side = unit_side(j)
        target, slot, sem = landing(place)
        return send(part.at[pl.ds(pl.multiple_of(block_row(place, side), sub), sub), :],
                    first_in.at[slot * 2 + side], first_send, first_recv.at[sem * 2 + side], target)

    def first_relay(j):
        @pl.when(middle == 1)
        def _():
            place = dest(j // 2)
            side = unit_side(j)
            row = pl.multiple_of(block_row(place, side), sub)
            wait_all(first_in.at[place * 2 + side], first_recv.at[place * 2 + side])
            def add(r, carry):
                at = pl.ds(pl.multiple_of(r * step_rows, step_rows), step_rows)
                mine_at = pl.ds(pl.multiple_of(row + r * step_rows, step_rows), step_rows)
                part[mine_at, :] = (
                    part[mine_at, :].astype(F32) + first_in[place * 2 + side, at, :].astype(F32)).astype(BF16)
                return carry
            lax.fori_loop(0, sub // step_rows, add, 0)
            first_copy(j).start()

    swap_copy = send(part.at[pl.ds(pl.multiple_of(block_row(z, 1 - x), sub), sub), :], swap_in,
                     swap_sem.at[0], swap_sem.at[1], partner)

    def first_wait(side):
        @pl.when(after_first == 1)
        def _():
            wait_all(first_in.at[zs * 2 + side], first_recv.at[zs * 2 + side])
        @pl.when(before_last == 1)
        def _():
            wait_all(first_in.at[(zs + 1) * 2 + side], first_recv.at[z * 2 + side])
        left = after_first * (zs * 2 + side) + (1 - after_first) * z * 2
        right = before_last * ((zs + 1) * 2 + side) + (1 - before_last) * z * 2
        return left, right

    def first_swap():
        row = block_row(z, 1 - x)
        left, right = first_wait(1 - x)
        def add(r, carry):
            at = pl.ds(pl.multiple_of(r * step_rows, step_rows), step_rows)
            mine_at = pl.ds(pl.multiple_of(row + r * step_rows, step_rows), step_rows)
            total = part[mine_at, :].astype(F32) + first_in[left, at, :].astype(F32)
            part[mine_at, :] = (total + first_in[right, at, :].astype(F32)).astype(BF16)
            return carry
        lax.fori_loop(0, sub // step_rows, add, 0)
        swap_copy.start()

    def first_finish(square):
        row = block_row(z, x)
        left, right = first_wait(x)
        swap_copy.wait_recv()
        def add(r, carry):
            at = pl.ds(pl.multiple_of(r * step_rows, step_rows), step_rows)
            mine_at = pl.ds(pl.multiple_of(row + r * step_rows, step_rows), step_rows)
            total = part[mine_at, :].astype(F32) + first_in[left, at, :].astype(F32)
            total = total + first_in[right, at, :].astype(F32) + swap_in[at, :].astype(F32)
            head_v[at, :] = total
            return carry + jnp.sum((total * total).reshape(step_rows // 8, 8, emit), axis=0)
        square = lax.fori_loop(0, sub // step_rows, add, square)
        pltpu.make_async_copy(head_v.at[pl.ds(0, sub), :], head_out.at[pl.ds(0, sub), :], out_sem).start()
        return square

    pre_copy(0, 0, 0).wait()
    step = 64
    for c, copy in enumerate(delta_copies):
        copy.wait()
        def narrow(r, carry):
            at = pl.ds(pl.multiple_of(c * chunk + r * step, step), step)
            low[at, :] = delta_v[at, :].astype(BF16)
            return carry
        lax.fori_loop(0, chunk // step, narrow, 0)
        at = pl.ds(c * chunk, chunk)
        p = pre_v[0, at, pl.ds(0, piece)].astype(F32)
        hidden = (p * jax.nn.sigmoid(p)).astype(BF16)
        value = lax.dot_general(hidden, low[at, :], (((0,), (0,)), ((), ())), preferred_element_type=F32)
        if c > 0:
            value = value + head_v[pl.ds(0, piece), :]
        if c < len(delta_copies) - 1:
            head_v[pl.ds(0, piece), :] = value
        else:
            part[pl.ds(pl.multiple_of(unit_row(0), piece), piece), :] = value.astype(BF16)

    pl.semaphore_wait(barrier, devices - 1)

    ready = piece // sub - 1
    @pl.when(middle == 0)
    def _():
        first_copy(0).start()
    for i in range(min(ready, q)):
        pair_copy(i).start()
    line_in[z * q] = jnp.zeros((sub, emit), BF16)
    first_in[z * 2] = jnp.zeros((sub, emit), BF16)

    wait_all(pre_v.at[pl.ds(0, firsts - 1), :, pl.ds(0, piece)], pre_sem.at[1])
    def opening(u, carry):
        product(u, 0)
        @pl.when(middle == 0)
        def _():
            first_copy(u).start()
        return carry
    lax.fori_loop(1, firsts, opening, 0)
    wait_all(pre_v.at[pl.ds(0, (2 * zs * hq - firsts) // hq)], pre_sem.at[2])
    if hq > 1:
        def second(t, carry):
            product(t // (hq - 1), 1 + t % (hq - 1))
            return carry
        lax.fori_loop(0, 3 * (hq - 1), second, 0)
    def more_pairs(i, carry):
        pair_copy(i).start()
        return carry
    lax.fori_loop(min(ready, q), lead, more_pairs, 0)
    first_relay(0)
    first_relay(1)
    weight_copy.wait()

    ids_copy.wait()
    for d in range(1, n):
        send(ids_all.at[me], ids_all.at[me], ids_send, ids_recv, lax.rem(me + d, n)).start()

    base = 3 + middle * (slopes - 8)
    stride = 3 - middle
    def main(t, carry):
        slope_sums(t)
        @pl.when((t >= 4) & (t % 2 == 0) & (t // 2 < firsts))
        def _():
            first_relay(t // 2)
        @pl.when((t >= base) & ((t - base) % stride == 0))
        def _():
            relay((t - base) // stride)
        return carry
    lax.fori_loop(0, slopes, main, 0)

    for d in range(1, heads):
        target = lax.rem(my_head + d, heads)
        pltpu.make_async_remote_copy(
            src_ref=small.at[target], dst_ref=small_in.at[lax.rem(my_head - target + heads, heads) - 1],
            send_sem=head_send, recv_sem=head_recv, device_id={"head": target}, device_id_type=MESH).start()

    done = slopes // 2
    if done < firsts:
        def rest_first(j, carry):
            first_relay(j)
            return carry
        lax.fori_loop(done, firsts, rest_first, 0)

    def add_rows(r, total):
        value = delta_v[pl.ds(pl.multiple_of(r * step, step), step), :]
        return total + jnp.sum(value.reshape(step // 8, 8, emit), axis=0)
    bias = lax.fori_loop(0, rows // step, add_rows, jnp.zeros((8, emit), F32))
    bias = jnp.sum(bias, axis=0, keepdims=True)
    pad = mine.shape[1] - spans
    tail = jnp.where(
        lax.broadcasted_iota(jnp.int32, (pad, emit), 0) == 0, jnp.broadcast_to(bias, (pad, emit)), 0.0
    ).astype(BF16)
    for h in range(2):
        mine[h, pl.ds(spans, pad), :] = tail[:, h * half:(h + 1) * half]

    ends = [(slopes - 4) // 3 + 1] + [(slopes - 4) // 3 + 1 + k for k in (2, 4, 5, 9, 11, 14)]
    inner = [3] + [3 + k for k in (1, 2, 4, 7, 9, 12)]
    stops = [(1 - middle) * e + middle * i for e, i in zip(ends, inner)] + [relays]

    if hq > 1:
        def third(t, carry):
            product(3 + t // (hq - 1), 1 + t % (hq - 1))
            return carry
        lax.fori_loop(0, (2 * zs - 5) * (hq - 1), third, 0)
    relay_range(stops[0], stops[1])
    def fourth(t, carry):
        product(2 * zs - 2 + t // hq, t % hq)
        return carry
    lax.fori_loop(0, 2 * hq, fourth, 0)
    first_swap()
    relay_range(stops[1], stops[2])
    relay_range(stops[2], stops[3])

    wait_all(small_in, head_recv)
    total = small[my_head].astype(F32)
    for d in range(heads - 1):
        total = total + small_in[d].astype(F32)
    for h in range(2):
        mine[h, pl.ds(0, spans), :] = total[:spans, h * half:(h + 1) * half].astype(BF16)
    embed_all[z, x] = total[spans:].astype(BF16)

    embed_pair = send(embed_all.at[z, x], embed_all.at[z, x], embed_pair_sem.at[0], embed_pair_sem.at[1], partner)
    embed_pair.start()

    roots = [zs // 2 - 1, zs // 2]
    def span_copy(h, right):
        return send(mine.at[h], span_in.at[h, 1 - right], span_send.at[h], span_recv.at[2 * h + 1 - right],
                    (z + 2 * right - 1) * 2 + x)
    def span_arrival(h, side):
        wait_all(span_in.at[h, side], span_recv.at[2 * h + side])
    for h in range(2):
        @pl.when(z == 0)
        def _():
            if roots[h] != 0:
                span_copy(h, 1).start()
        @pl.when(z == zs - 1)
        def _():
            if roots[h] != zs - 1:
                span_copy(h, 0).start()

    relay_range(stops[3], stops[4])

    def embed_copy(j, right):
        source = z + j - 2 * right * j
        return send(embed_all.at[source], embed_all.at[source], embed_send.at[right], embed_recv.at[source],
                    (z + 2 * right - 1) * 2 + x)

    def embed_step(j):
        if j > 0:
            @pl.when((z - (j - 1) >= 0) & (z < zs - 1))
            def _():
                embed_copy(j - 1, 1).wait_send()
            @pl.when((z + j - 1 <= zs - 1) & (z > 0))
            def _():
                embed_copy(j - 1, 0).wait_send()
            @pl.when(z - j >= 0)
            def _():
                wait_all(embed_all.at[z - j], embed_recv.at[z - j])
            @pl.when(z + j <= zs - 1)
            def _():
                wait_all(embed_all.at[z + j], embed_recv.at[z + j])
        if j < zs - 1:
            @pl.when((z - j >= 0) & (z < zs - 1))
            def _():
                embed_copy(j, 1).start()
            @pl.when((z + j <= zs - 1) & (z > 0))
            def _():
                embed_copy(j, 0).start()

    embed_pair.wait_recv()
    for h in range(2):
        for right, between in ((1, (z > 0) & (z < roots[h])), (0, (z < zs - 1) & (z > roots[h]))):
            @pl.when(between)
            def _():
                span_arrival(h, 1 - right)
                mine[h] = (mine[h].astype(F32) + span_in[h, 1 - right].astype(F32)).astype(BF16)
                span_copy(h, right).start()
    embed_step(0)

    relay_range(stops[4], stops[5])

    span_pair_copy = send(span_part, span_pair, span_pair_sem.at[0], span_pair_sem.at[1], partner)
    for h in range(2):
        @pl.when(z == roots[h])
        def _():
            total = mine[h].astype(F32)
            for side, there in ((0, roots[h] > 0), (1, roots[h] < zs - 1)):
                if there:
                    span_arrival(h, side)
                    total = total + span_in[h, side].astype(F32)
            span_part[...] = total.astype(BF16)
            span_pair_copy.start()
    embed_step(1)

    relay_range(stops[5], stops[6])

    def all_copy(h, d):
        return send(span_all.at[h], span_all.at[h], all_send, all_recv.at[h], lax.rem(z + d, zs) * 2 + x)
    for h in range(2):
        @pl.when(z == roots[h])
        def _():
            span_pair_copy.wait_recv()
            span_all[h] = (span_part[...].astype(F32) + span_pair[...].astype(F32)).astype(BF16)
            for d in range(1, zs):
                all_copy(h, d).start()
    for j in range(2, zs):
        embed_step(j)

    relay_range(stops[6], stops[7])
    square = jnp.zeros((8, emit), F32)
    square = first_finish(square)
    square = lax.fori_loop(0, 3, finish, square)

    wait_all(ids_all.at[pl.ds(0, n - 1)], ids_recv)
    wanted = lax.broadcasted_iota(jnp.int32, (clients, clients), 0) + me * clients
    embed_raw = jnp.zeros((clients, emit), F32)
    for c in range(n):
        chosen = (jnp.broadcast_to(ids_all[c], (clients, clients)) == wanted).astype(F32).astype(BF16)
        embed_raw = embed_raw + jnp.dot(chosen, embed_all[c // 2, c % 2], preferred_element_type=F32)
    embed_v[...] = embed_raw
    embed_write = pltpu.make_async_copy(embed_v, embed_out, write_sem.at[0])
    embed_write.start()
    embed_square = jnp.sum(embed_raw * embed_raw)

    rest_square = jnp.zeros((), F32)
    for h in range(2):
        @pl.when(z != roots[h])
        def _():
            wait_all(span_all.at[h], all_recv.at[h])
        value = span_all[h].astype(F32)
        rest_v[:, pl.ds(h * half, half)] = value
        rest_square = rest_square + jnp.sum(value * value)
    rest_write = pltpu.make_async_copy(rest_v, rest_out, write_sem.at[1])
    rest_write.start()

    square = lax.fori_loop(3, q, finish, square)
    head_total = jnp.sum(square)

    lane = lax.broadcasted_iota(jnp.int32, (1, 128), 1)
    stat_all[flat] = jnp.where(lane == 0, head_total, jnp.where(lane == 1, embed_square, rest_square / n))
    def tell(d, carry):
        pltpu.make_async_remote_copy(
            src_ref=stat_all.at[flat], dst_ref=stat_all.at[flat], send_sem=stat_send,
            recv_sem=stat_recv, device_id=device(d), device_id_type=MESH).start()
        return carry
    lax.fori_loop(1, devices, tell, 0)

    wait_all(part.at[pl.ds(0, zs * q * sub)], pair_send)
    for i in range(relays - queue, relays):
        line_copy(i).wait_send()
    wait_all(part.at[pl.ds(0, firsts * sub)], first_send)
    swap_copy.wait_send()
    embed_pair.wait_send()
    wait_all(small.at[pl.ds(0, heads - 1)], head_send)
    wait_all(ids_all.at[pl.ds(0, n - 1)], ids_send)
    for h in range(2):
        @pl.when(z < roots[h])
        def _():
            span_copy(h, 1).wait_send()
        @pl.when(z > roots[h])
        def _():
            span_copy(h, 0).wait_send()
        @pl.when(z == roots[h])
        def _():
            span_pair_copy.wait_send()
            wait_all(part.at[pl.ds(0, (zs - 1) * mine.shape[1] // 2)], all_send)
    embed_write.wait()
    rest_write.wait()
    pltpu.make_async_copy(head_v, head_out, out_sem).wait()

    wait_all(stat_all.at[pl.ds(0, devices - 1)], stat_recv)
    stat_out[...] = jnp.sum(stat_all[...], axis=0)
    wait_all(stat_all.at[pl.ds(0, devices - 1)], stat_send)


def scale_kernel(sizes, stat_ref, head_ref, rest_ref, embed_ref, head_out, bias_out, embed_out, span_out,
                 stat, head, rest, embed, in_sem, out_sem):
    head_size, embed_size, rest_size = sizes
    spans = span_out.shape[0]
    steps = in_sem.shape[0] - 3
    rows = head.shape[0] // steps
    stat_in = pltpu.make_async_copy(stat_ref, stat, in_sem.at[steps])
    rest_in = pltpu.make_async_copy(rest_ref, rest, in_sem.at[steps + 1])
    embed_in = pltpu.make_async_copy(embed_ref, embed, in_sem.at[steps + 2])
    def part(ref, i):
        return ref.at[pl.ds(i * rows, rows), :]
    stat_in.start()
    heads_in = [pltpu.make_async_copy(part(head_ref, i), part(head, i), in_sem.at[i]) for i in range(steps)]
    heads_out = [pltpu.make_async_copy(part(head, i), part(head_out, i), out_sem.at[i]) for i in range(steps)]
    for copy in heads_in:
        copy.start()
    rest_in.start()
    embed_in.start()
    stat_in.wait()
    factor = clip_factor(stat[0:1, 0:1], head_size)
    embed_factor = clip_factor(stat[0:1, 1:2], embed_size)
    rest_factor = clip_factor(stat[0:1, 2:3], rest_size)
    for i in range(steps):
        heads_in[i].wait()
        head[pl.ds(i * rows, rows), :] = factor * head[pl.ds(i * rows, rows), :]
        heads_out[i].start()
    rest_in.wait()
    rest[...] = rest_factor * rest[...]
    bias_copy = pltpu.make_async_copy(rest.at[pl.ds(spans, 1), :], bias_out, out_sem.at[steps])
    span_copy = pltpu.make_async_copy(rest.at[pl.ds(0, spans), :], span_out, out_sem.at[steps + 1])
    bias_copy.start()
    span_copy.start()
    embed_in.wait()
    embed[...] = embed_factor * embed[...]
    embed_copy = pltpu.make_async_copy(embed, embed_out, out_sem.at[steps + 2])
    embed_copy.start()
    for copy in heads_out + [bias_copy, span_copy, embed_copy]:
        copy.wait()


def per_device(n, heads, pre, delta, head_weight, client_ids):
    rows, hidden_width = pre.shape
    emit = delta.shape[1]
    clients = client_ids.shape[0]
    spans = rows // clients
    block = hidden_width // n
    piece = min(256, block)
    hq = block // piece
    zs = n // 2
    q = 7
    sub = block // (q + 1)
    padded = (spans + 16) // 16 * 16
    half = emit // 2
    cfg = (n, heads, block, piece, spans, clients)
    ids = client_ids.reshape(1, clients)
    hbm = pl.BlockSpec(memory_space=pl.ANY)
    vmem = pl.BlockSpec(memory_space=pltpu.VMEM)
    dma = pltpu.SemaphoreType.DMA
    chunk = math.gcd(rows, 256)
    head_raw, rest_raw, embed_raw, stats = pl.pallas_call(
        functools.partial(kernel, cfg),
        out_shape=(
            jax.ShapeDtypeStruct((block, emit), F32),
            jax.ShapeDtypeStruct((padded, emit), F32),
            jax.ShapeDtypeStruct((clients, emit), F32),
            jax.ShapeDtypeStruct((1, 128), F32),
        ),
        in_specs=[hbm, hbm, hbm, hbm],
        out_specs=(hbm, hbm, hbm, vmem),
        scratch_shapes=[
            pltpu.VMEM((n, rows, block), BF16),
            pltpu.VMEM((rows, emit), F32),
            pltpu.VMEM((rows, emit), BF16),
            pltpu.VMEM((hidden_width, emit), BF16),
            pltpu.VMEM((hidden_width, emit), BF16),
            pltpu.VMEM((zs * q, sub, emit), BF16),
            pltpu.VMEM(((zs + 2) * q, sub, emit), BF16),
            pltpu.VMEM(((zs + 2) * 2, sub, emit), BF16),
            pltpu.VMEM((sub, emit), BF16),
            pltpu.VMEM((block, emit), F32),
            pltpu.VMEM((heads, spans + clients, emit), BF16),
            pltpu.VMEM((heads - 1, spans + clients, emit), BF16),
            pltpu.VMEM((2, padded, half), BF16),
            pltpu.VMEM((2, 2, padded, half), BF16),
            pltpu.VMEM((padded, half), BF16),
            pltpu.VMEM((padded, half), BF16),
            pltpu.VMEM((2, padded, half), BF16),
            pltpu.VMEM((zs, 2, clients, emit), BF16),
            pltpu.VMEM((n, 1, clients), jnp.int32),
            pltpu.VMEM((clients, emit), F32),
            pltpu.VMEM((padded, emit), F32),
            pltpu.VMEM((n * heads, 1, 128), F32),
            dma((3,)), dma((rows // chunk,)), dma, dma,
            dma, dma((zs * q,)), dma((3,)), dma(((zs + 1) * q,)),
            dma, dma(((zs + 1) * 2,)), dma((2,)), dma, dma,
            dma((2,)), dma((4,)), dma((2,)), dma, dma((2,)), dma((2,)), dma((2,)), dma((2,)), dma((zs,)),
            dma, dma, dma, dma, dma,
        ],
        compiler_params=pltpu.CompilerParams(
            collective_id=0, has_side_effects=True, vmem_limit_bytes=62 * 2**20
        ),
        name="clipped_grads",
    )(pre, delta, head_weight, ids)
    sizes = (hidden_width * emit * heads, clients * n * hidden_width, spans * hidden_width + emit * heads)
    steps = 4
    head_grad, bias_grad, embed_grad, span_grad = pl.pallas_call(
        functools.partial(scale_kernel, sizes),
        out_shape=(
            jax.ShapeDtypeStruct((block, emit), F32),
            jax.ShapeDtypeStruct((1, emit), F32),
            jax.ShapeDtypeStruct((clients, emit), F32),
            jax.ShapeDtypeStruct((spans, emit), F32),
        ),
        in_specs=[hbm] * 4,
        out_specs=(hbm,) * 4,
        scratch_shapes=[
            pltpu.VMEM((1, 128), F32),
            pltpu.VMEM((block, emit), F32),
            pltpu.VMEM((padded, emit), F32),
            pltpu.VMEM((clients, emit), F32),
            dma((steps + 3,)), dma((steps + 3,)),
        ],
        name="scaled",
    )(stats, head_raw, rest_raw, embed_raw)
    return head_grad, bias_grad.reshape(emit), embed_grad, span_grad


def solution(mesh):
    placed = (P("client", None), P("client", "head"), P(None, "head"), P("client"))
    return jax.shard_map(
        functools.partial(per_device, mesh.shape["client"], mesh.shape["head"]),
        mesh=mesh,
        in_specs=placed,
        out_specs=(P("client", "head"), P("head"), P("client", "head"), P(None, "head")),
        check_vma=False,
    )
```

time: 109 us -> 112 us (1.028)
  Pallas kernels: 108 us -> 111 us
    pallas_call x1, Pallas kernels: 105 us -> 109 us  [per_device(): pl.pallas_call(functools.partial(kernel, cfg), out_shape=(jax.ShapeDtypeS...]
where the time goes in v3:
time: 112 us
  Pallas kernels  111 us (99%)
    pallas_call x1, Pallas kernels, per_device(): pl.pallas_call(functools.partial(kernel, cfg), out_shape=(jax.ShapeDtypeS...  109 us
    pallas_call x1, Pallas kernels, per_device(): pl.pallas_call(functools.partial(scale_kernel, sizes), out_shape=(jax.Sha...  2.7 us

profile of v3, /device:TPU:0, one launch (start us, length us, event | category | flops | bytes accessed | tf_op | source)
XLA Modules:
  0.0 112.0 jit_solution(15221513454126287190)
XLA Ops:
  0.6 108.6 %clipped_grads.1 = (f32[512,1024]{1,0:T(8,128)}, f32[96,1024]{1,0:T(8,128)}, f32[16,1024]{1,0:T(8,128)}, f32[1,128]{1,0:T(1,128)}) custom-call(bf16[1280,4096]{1,0:T(8,128)(2,1)} %pre_ref.1, f32[1280,1024]{1,0:T(8,128)} %delta_ref.1, bf16[4096,1024]{1,0:T(8,128)(2,1)} %weight_ref.1, s32[1,16]{1,0:T(1,128)} %bitcast.2), custom_call_target="tpu_custom_call" | custom-call | tf_op jit(solution)/shard_map/clipped_grads/pallas_call | solution.py:617
  109.3 2.7 %scaled.1 = (f32[512,1024]{1,0:T(8,128)}, f32[1,1024]{1,0:T(1,128)}, f32[16,1024]{1,0:T(8,128)}, f32[80,1024]{1,0:T(8,128)}) custom-call(f32[1,128]{1,0:T(1,128)} %get-tuple-element.12.stat_ref, f32[512,1024]{1,0:T(8,128)} %get-tuple-element.13.head_ref, f32[96,1024]{1,0:T(8,128)} %get-tuple-element.14.rest_ref, f32[16,1024]{1,0:T(8,128)} %get-tuple-element.15.embed_ref), custom_call_target="tpu_custom_call" | custom-call | tf_op jit(solution)/shard_map/scaled/pallas_call | solution.py:663

commit v4 on v3

--- a/solution.py
+++ b/solution.py
@@ -159,10 +159,10 @@
         return send(part.at[pl.ds(piece_row(place, x, i % q), sub), :], line_in.at[slot * q + i % q],
                     line_send.at[i % queue], line_recv.at[sem * q + i % q], target)
 
-    lead = q + 4 * middle
+    lead = q + 2 * middle
     step_rows = min(32, sub)
 
-    def relay(i):
+    def relay(i, ahead):
         place = dest(i // q)
         row = piece_row(place, x, i % q)
         pair_copy(i).wait_recv()
@@ -181,13 +181,13 @@
         def _():
             line_copy(i - queue).wait_send()
         line_copy(i).start()
-        @pl.when(i + lead < zs * q)
-        def _():
-            pair_copy(i + lead).start()
-
-    def relay_range(start, stop):
+        @pl.when(i + ahead < zs * q)
+        def _():
+            pair_copy(i + ahead).start()
+
+    def relay_range(start, stop, ahead):
         def body(i, carry):
-            relay(i)
+            relay(i, ahead)
             return carry
         lax.fori_loop(start, stop, body, 0)
 
@@ -346,7 +346,7 @@
             first_relay(t // 2)
         @pl.when((t >= base) & ((t - base) % stride == 0))
         def _():
-            relay((t - base) // stride)
+            relay((t - base) // stride, lead)
         return carry
     lax.fori_loop(0, slopes, main, 0)
 
@@ -375,8 +375,8 @@
     for h in range(2):
         mine[h, pl.ds(spans, pad), :] = tail[:, h * half:(h + 1) * half]
 
-    ends = [(slopes - 4) // 3 + 1] + [(slopes - 4) // 3 + 1 + k for k in (2, 4, 5, 9, 11, 14)]
-    inner = [3] + [3 + k for k in (1, 2, 4, 7, 9, 12)]
+    ends = [(slopes - 4) // 3 + 1] + [(slopes - 4) // 3 + 1 + k for k in (2, 4, 4, 8, 13, 16)]
+    inner = [3] + [3 + k for k in (1, 2, 3, 7, 11, 15)]
     stops = [(1 - middle) * e + middle * i for e, i in zip(ends, inner)] + [relays]
 
     if hq > 1:
@@ -384,14 +384,13 @@
             product(3 + t // (hq - 1), 1 + t % (hq - 1))
             return carry
         lax.fori_loop(0, (2 * zs - 5) * (hq - 1), third, 0)
-    relay_range(stops[0], stops[1])
+    relay_range(stops[0], stops[1], lead)
     def fourth(t, carry):
         product(2 * zs - 2 + t // hq, t % hq)
         return carry
     lax.fori_loop(0, 2 * hq, fourth, 0)
-    first_swap()
-    relay_range(stops[1], stops[2])
-    relay_range(stops[2], stops[3])
+    relay_range(stops[1], stops[2], lead)
+    relay_range(stops[2], stops[3], lead)
 
     wait_all(small_in, head_recv)
     total = small[my_head].astype(F32)
@@ -403,6 +402,10 @@
 
     embed_pair = send(embed_all.at[z, x], embed_all.at[z, x], embed_pair_sem.at[0], embed_pair_sem.at[1], partner)
     embed_pair.start()
+    @pl.when(middle == 1)
+    def _():
+        pair_copy(stops[3] + lead).start()
+    lead = lead + middle
 
     roots = [zs // 2 - 1, zs // 2]
     def span_copy(h, right):
@@ -420,7 +423,7 @@
             if roots[h] != zs - 1:
                 span_copy(h, 0).start()
 
-    relay_range(stops[3], stops[4])
+    relay_range(stops[3], stops[4], lead)
 
     def embed_copy(j, right):
         source = z + j - 2 * right * j
@@ -428,26 +431,14 @@
                     (z + 2 * right - 1) * 2 + x)
 
     def embed_step(j):
-        if j > 0:
-            @pl.when((z - (j - 1) >= 0) & (z < zs - 1))
+        for right, near_end, there in ((1, before_last, z - j >= 0), (0, after_first, z + j <= zs - 1)):
+            @pl.when((near_end == 1) & there)
             def _():
-                embed_copy(j - 1, 1).wait_send()
-            @pl.when((z + j - 1 <= zs - 1) & (z > 0))
-            def _():
-                embed_copy(j - 1, 0).wait_send()
-            @pl.when(z - j >= 0)
-            def _():
-                wait_all(embed_all.at[z - j], embed_recv.at[z - j])
-            @pl.when(z + j <= zs - 1)
-            def _():
-                wait_all(embed_all.at[z + j], embed_recv.at[z + j])
-        if j < zs - 1:
-            @pl.when((z - j >= 0) & (z < zs - 1))
-            def _():
-                embed_copy(j, 1).start()
-            @pl.when((z + j <= zs - 1) & (z > 0))
-            def _():
-                embed_copy(j, 0).start()
+                if j > 0:
+                    source = z + j - 2 * right * j
+                    wait_all(embed_all.at[source], embed_recv.at[source])
+                    embed_copy(j - 1, right).wait_send()
+                embed_copy(j, right).start()
 
     embed_pair.wait_recv()
     for h in range(2):
@@ -459,7 +450,7 @@
                 span_copy(h, right).start()
     embed_step(0)
 
-    relay_range(stops[4], stops[5])
+    relay_range(stops[4], stops[5], lead)
 
     span_pair_copy = send(span_part, span_pair, span_pair_sem.at[0], span_pair_sem.at[1], partner)
     for h in range(2):
@@ -472,9 +463,10 @@
                     total = total + span_in[h, side].astype(F32)
             span_part[...] = total.astype(BF16)
             span_pair_copy.start()
+    first_swap()
     embed_step(1)
 
-    relay_range(stops[5], stops[6])
+    relay_range(stops[5], stops[6], lead)
 
     def all_copy(h, d):
         return send(span_all.at[h], span_all.at[h], all_send, all_recv.at[h], lax.rem(z + d, zs) * 2 + x)
@@ -485,14 +477,25 @@
             span_all[h] = (span_part[...].astype(F32) + span_pair[...].astype(F32)).astype(BF16)
             for d in range(1, zs):
                 all_copy(h, d).start()
-    for j in range(2, zs):
+    for j in range(2, zs - 1):
         embed_step(j)
 
-    relay_range(stops[6], stops[7])
+    relay_range(stops[6], stops[7], lead)
     square = jnp.zeros((8, emit), F32)
     square = first_finish(square)
-    square = lax.fori_loop(0, 3, finish, square)
-
+    square = lax.fori_loop(0, 5, finish, square)
+
+    for j in range(1, zs):
+        for right, near_end, there in ((1, before_last, z - j >= 0), (0, after_first, z + j <= zs - 1)):
+            source = z + j - 2 * right * j
+            @pl.when(there if j == zs - 1 else (near_end == 0) & there)
+            def _():
+                wait_all(embed_all.at[source], embed_recv.at[source])
+    for right, near_end, last in ((1, before_last, z), (0, after_first, zs - 1 - z)):
+        for j in range(zs - 1):
+            @pl.when((near_end == 1) & (last == j))
+            def _():
+                embed_copy(j, right).wait_send()
     wait_all(ids_all.at[pl.ds(0, n - 1)], ids_recv)
     wanted = lax.broadcasted_iota(jnp.int32, (clients, clients), 0) + me * clients
     embed_raw = jnp.zeros((clients, emit), F32)
@@ -515,7 +518,7 @@
     rest_write = pltpu.make_async_copy(rest_v, rest_out, write_sem.at[1])
     rest_write.start()
 
-    square = lax.fori_loop(3, q, finish, square)
+    square = lax.fori_loop(5, q, finish, square)
     head_total = jnp.sum(square)
 
     lane = lax.broadcasted_iota(jnp.int32, (1, 128), 1)

time: 112 us -> 105 us (0.938)
  Pallas kernels: 111 us -> 105 us
    pallas_call x1, Pallas kernels: 109 us -> 102 us  [per_device(): pl.pallas_call(functools.partial(kernel, cfg), out_shape=(jax.ShapeDtypeS...]
where the time goes in v4:
time: 105 us
  Pallas kernels  105 us (100%)
    pallas_call x1, Pallas kernels, per_device(): pl.pallas_call(functools.partial(kernel, cfg), out_shape=(jax.ShapeDtypeS...  102 us
    pallas_call x1, Pallas kernels, per_device(): pl.pallas_call(functools.partial(scale_kernel, sizes), out_shape=(jax.Sha...  2.7 us

profile of v4, /device:TPU:0, one launch (start us, length us, event | category | flops | bytes accessed | tf_op | source)
XLA Modules:
  0.0 105.3 jit_solution(18228242791383851053)
XLA Ops:
  0.6 102.0 %clipped_grads.1 = (f32[512,1024]{1,0:T(8,128)}, f32[96,1024]{1,0:T(8,128)}, f32[16,1024]{1,0:T(8,128)}, f32[1,128]{1,0:T(1,128)}) custom-call(bf16[1280,4096]{1,0:T(8,128)(2,1)} %pre_ref.1, f32[1280,1024]{1,0:T(8,128)} %delta_ref.1, bf16[4096,1024]{1,0:T(8,128)(2,1)} %weight_ref.1, s32[1,16]{1,0:T(1,128)} %bitcast.2), custom_call_target="tpu_custom_call" | custom-call | tf_op jit(solution)/shard_map/clipped_grads/pallas_call | solution.py:620
  102.6 2.7 %scaled.1 = (f32[512,1024]{1,0:T(8,128)}, f32[1,1024]{1,0:T(1,128)}, f32[16,1024]{1,0:T(8,128)}, f32[80,1024]{1,0:T(8,128)}) custom-call(f32[1,128]{1,0:T(1,128)} %get-tuple-element.12.stat_ref, f32[512,1024]{1,0:T(8,128)} %get-tuple-element.13.head_ref, f32[96,1024]{1,0:T(8,128)} %get-tuple-element.14.rest_ref, f32[16,1024]{1,0:T(8,128)} %get-tuple-element.15.embed_ref), custom_call_target="tpu_custom_call" | custom-call | tf_op jit(solution)/shard_map/scaled/pallas_call | solution.py:666

commit v5 on v4

--- a/solution.py
+++ b/solution.py
@@ -22,7 +22,7 @@
            pre_v, delta_v, low, weight_v, part, pair_in, line_in, first_in, swap_in, head_v,
            small, small_in, mine, span_in, span_part, span_pair, span_all, embed_all, ids_all,
            embed_v, rest_v, stat_all,
-           pre_sem, delta_sem, weight_sem, out_sem, pair_send, pair_recv, line_send, line_recv,
+           pre_sem, first_pre_sem, delta_sem, weight_sem, out_sem, pair_send, pair_recv, line_send, line_recv,
            first_send, first_recv, swap_sem, head_send, head_recv, span_send, span_recv, span_pair_sem,
            all_send, all_recv, write_sem, embed_pair_sem, embed_send, embed_recv, ids_sem, ids_send, ids_recv,
            stat_send, stat_recv):
@@ -97,34 +97,41 @@
         for c in range(rows // chunk)]
     weight_copy = pltpu.make_async_copy(weight_ref, weight_v, weight_sem)
     ids_copy = pltpu.make_async_copy(ids_ref, ids_all.at[me], ids_sem)
-    pre_copy(0, 0, 0).start()
-    for copy in delta_copies:
-        copy.start()
-
-    def device(d):
-        other = lax.rem(flat + d, devices)
-        return {"client": other // heads, "head": other % heads}
+    first_column = pl.multiple_of(unit_row(0), piece)
+    first_copies = [
+        pltpu.make_async_copy(pre_ref.at[pl.ds(c * chunk, chunk), pl.ds(first_column, piece)],
+                              pre_v.at[0, pl.ds(c * chunk, chunk), pl.ds(0, piece)], first_pre_sem.at[c])
+        for c in range(rows // chunk)]
+    for c in range(rows // chunk):
+        first_copies[c].start()
+        delta_copies[c].start()
+
+    def each_other(action):
+        columns = [lax.rem(my_head + d, heads) for d in range(heads)]
+        for column in columns[1:]:
+            action(me, column)
+        def body(d, carry):
+            client = lax.rem(me + d, n)
+            for column in columns:
+                action(client, column)
+            return carry
+        lax.fori_loop(1, n, body, 0)
 
     barrier = pltpu.get_barrier_semaphore()
-    def greet(d, carry):
-        pl.semaphore_signal(barrier, inc=1, device_id=device(d), device_id_type=MESH)
+    def greet(client, head):
+        pl.semaphore_signal(barrier, inc=1, device_id={"client": client, "head": head}, device_id_type=MESH)
+    each_other(greet)
+
+    def load(u, carry):
+        pre_copy(u, 0, 0).start()
         return carry
-    lax.fori_loop(1, devices, greet, 0)
-
-    def load(u, carry):
-        pre_copy(u, 0, 1).start()
-        return carry
-    lax.fori_loop(1, firsts, load, 0)
     def load_rest(u, carry):
         @pl.when(u >= firsts)
         def _():
-            pre_copy(u, 0, 2).start()
+            pre_copy(u, 0, 1).start()
         for h in range(1, hq):
-            pre_copy(u, h, 2).start()
+            pre_copy(u, h, 1).start()
         return carry
-    lax.fori_loop(0 if hq > 1 else firsts, 2 * zs, load_rest, 0)
-    weight_copy.start()
-    ids_copy.start()
 
     def product(u, h):
         p = pre_v[u, :, pl.ds(pl.multiple_of(h * piece, piece), piece)].astype(F32)
@@ -151,18 +158,37 @@
         return send(part.at[pl.ds(piece_row(dest(i // q), 1 - x, i % q), sub), :], pair_in.at[i],
                     pair_send, pair_recv.at[i], partner)
 
-    queue = 3
-
-    def line_copy(i):
+    queue = 3 + middle
+    swaps = 1 if zs == 4 else 0
+
+    def order(r):
+        m = r - q
+        late = swaps * middle * ((m + relays) // relays)
+        return late * (q + m % 2 * q + m // 2) + (1 - late) * r
+
+    def pairs_sent(r):
+        late = swaps * middle * ((r - q + relays) // relays)
+        return late * (2 * q + 2 + (r - q) // 2) + (1 - late) * (r + q + 2 * middle)
+
+    def line_copy(r):
+        i = order(r)
         place = dest(i // q)
         target, slot, sem = landing(place)
         return send(part.at[pl.ds(piece_row(place, x, i % q), sub), :], line_in.at[slot * q + i % q],
-                    line_send.at[i % queue], line_recv.at[sem * q + i % q], target)
-
-    lead = q + 2 * middle
+                    line_send.at[r % queue], line_recv.at[sem * q + i % q], target)
+
     step_rows = min(32, sub)
 
-    def relay(i, ahead):
+    def start_pairs(start, stop):
+        def body(i, carry):
+            @pl.when(i < zs * q)
+            def _():
+                pair_copy(i).start()
+            return carry
+        lax.fori_loop(start, stop, body, 0)
+
+    def relay(r, extra):
+        i = order(r)
         place = dest(i // q)
         row = piece_row(place, x, i % q)
         pair_copy(i).wait_recv()
@@ -177,17 +203,15 @@
             part[mine_at, :] = (total + line_in[slot, at, :].astype(F32)).astype(BF16)
             return carry
         lax.fori_loop(0, sub // step_rows, add, 0)
-        @pl.when(i >= queue)
-        def _():
-            line_copy(i - queue).wait_send()
-        line_copy(i).start()
-        @pl.when(i + ahead < zs * q)
-        def _():
-            pair_copy(i + ahead).start()
-
-    def relay_range(start, stop, ahead):
-        def body(i, carry):
-            relay(i, ahead)
+        @pl.when(r >= queue)
+        def _():
+            line_copy(r - queue).wait_send()
+        line_copy(r).start()
+        start_pairs(pairs_sent(r) + extra, pairs_sent(r + 1) + extra)
+
+    def relay_range(start, stop, extra):
+        def body(r, carry):
+            relay(r, extra)
             return carry
         lax.fori_loop(start, stop, body, 0)
 
@@ -280,10 +304,11 @@
         pltpu.make_async_copy(head_v.at[pl.ds(0, sub), :], head_out.at[pl.ds(0, sub), :], out_sem).start()
         return square
 
-    pre_copy(0, 0, 0).wait()
+    lax.fori_loop(1, firsts, load, 0)
     step = 64
-    for c, copy in enumerate(delta_copies):
-        copy.wait()
+    for c in range(rows // chunk):
+        first_copies[c].wait()
+        delta_copies[c].wait()
         def narrow(r, carry):
             at = pl.ds(pl.multiple_of(c * chunk + r * step, step), step)
             low[at, :] = delta_v[at, :].astype(BF16)
@@ -308,10 +333,13 @@
         first_copy(0).start()
     for i in range(min(ready, q)):
         pair_copy(i).start()
+    lax.fori_loop(0 if hq > 1 else firsts, 2 * zs, load_rest, 0)
+    weight_copy.start()
+    ids_copy.start()
     line_in[z * q] = jnp.zeros((sub, emit), BF16)
     first_in[z * 2] = jnp.zeros((sub, emit), BF16)
 
-    wait_all(pre_v.at[pl.ds(0, firsts - 1), :, pl.ds(0, piece)], pre_sem.at[1])
+    wait_all(pre_v.at[pl.ds(0, firsts - 1), :, pl.ds(0, piece)], pre_sem.at[0])
     def opening(u, carry):
         product(u, 0)
         @pl.when(middle == 0)
@@ -319,16 +347,13 @@
             first_copy(u).start()
         return carry
     lax.fori_loop(1, firsts, opening, 0)
-    wait_all(pre_v.at[pl.ds(0, (2 * zs * hq - firsts) // hq)], pre_sem.at[2])
+    wait_all(pre_v.at[pl.ds(0, (2 * zs * hq - firsts) // hq)], pre_sem.at[1])
     if hq > 1:
         def second(t, carry):
             product(t // (hq - 1), 1 + t % (hq - 1))
             return carry
         lax.fori_loop(0, 3 * (hq - 1), second, 0)
-    def more_pairs(i, carry):
-        pair_copy(i).start()
-        return carry
-    lax.fori_loop(min(ready, q), lead, more_pairs, 0)
+    start_pairs(min(ready, q), pairs_sent(0))
     first_relay(0)
     first_relay(1)
     weight_copy.wait()
@@ -346,7 +371,7 @@
             first_relay(t // 2)
         @pl.when((t >= base) & ((t - base) % stride == 0))
         def _():
-            relay((t - base) // stride, lead)
+            relay((t - base) // stride, 0)
         return carry
     lax.fori_loop(0, slopes, main, 0)
 
@@ -376,7 +401,7 @@
         mine[h, pl.ds(spans, pad), :] = tail[:, h * half:(h + 1) * half]
 
     ends = [(slopes - 4) // 3 + 1] + [(slopes - 4) // 3 + 1 + k for k in (2, 4, 4, 8, 13, 16)]
-    inner = [3] + [3 + k for k in (1, 2, 3, 7, 11, 15)]
+    inner = [3] + [3 + k for k in (1, 2, 3, 8, 15, 18)]
     stops = [(1 - middle) * e + middle * i for e, i in zip(ends, inner)] + [relays]
 
     if hq > 1:
@@ -384,13 +409,13 @@
             product(3 + t // (hq - 1), 1 + t % (hq - 1))
             return carry
         lax.fori_loop(0, (2 * zs - 5) * (hq - 1), third, 0)
-    relay_range(stops[0], stops[1], lead)
+    relay_range(stops[0], stops[1], 0)
     def fourth(t, carry):
         product(2 * zs - 2 + t // hq, t % hq)
         return carry
     lax.fori_loop(0, 2 * hq, fourth, 0)
-    relay_range(stops[1], stops[2], lead)
-    relay_range(stops[2], stops[3], lead)
+    relay_range(stops[1], stops[2], 0)
+    relay_range(stops[2], stops[3], 0)
 
     wait_all(small_in, head_recv)
     total = small[my_head].astype(F32)
@@ -402,10 +427,6 @@
 
     embed_pair = send(embed_all.at[z, x], embed_all.at[z, x], embed_pair_sem.at[0], embed_pair_sem.at[1], partner)
     embed_pair.start()
-    @pl.when(middle == 1)
-    def _():
-        pair_copy(stops[3] + lead).start()
-    lead = lead + middle
 
     roots = [zs // 2 - 1, zs // 2]
     def span_copy(h, right):
@@ -423,7 +444,8 @@
             if roots[h] != zs - 1:
                 span_copy(h, 0).start()
 
-    relay_range(stops[3], stops[4], lead)
+    start_pairs(pairs_sent(stops[3]), pairs_sent(stops[3]) + middle)
+    relay_range(stops[3], stops[4], middle)
 
     def embed_copy(j, right):
         source = z + j - 2 * right * j
@@ -450,7 +472,7 @@
                 span_copy(h, right).start()
     embed_step(0)
 
-    relay_range(stops[4], stops[5], lead)
+    relay_range(stops[4], stops[5], middle)
 
     span_pair_copy = send(span_part, span_pair, span_pair_sem.at[0], span_pair_sem.at[1], partner)
     for h in range(2):
@@ -466,7 +488,8 @@
     first_swap()
     embed_step(1)
 
-    relay_range(stops[5], stops[6], lead)
+    start_pairs(pairs_sent(stops[5]) + middle, pairs_sent(stops[5]) + 3 * middle)
+    relay_range(stops[5], stops[6], 3 * middle)
 
     def all_copy(h, d):
         return send(span_all.at[h], span_all.at[h], all_send, all_recv.at[h], lax.rem(z + d, zs) * 2 + x)
@@ -480,7 +503,8 @@
     for j in range(2, zs - 1):
         embed_step(j)
 
-    relay_range(stops[6], stops[7], lead)
+    relay_range(stops[6], stops[7], 3 * middle)
+    start_pairs(pairs_sent(relays) + 3 * middle, zs * q)
     square = jnp.zeros((8, emit), F32)
     square = first_finish(square)
     square = lax.fori_loop(0, 5, finish, square)
@@ -523,16 +547,17 @@
 
     lane = lax.broadcasted_iota(jnp.int32, (1, 128), 1)
     stat_all[flat] = jnp.where(lane == 0, head_total, jnp.where(lane == 1, embed_square, rest_square / n))
-    def tell(d, carry):
+    def tell(client, head):
         pltpu.make_async_remote_copy(
-            src_ref=stat_all.at[flat], dst_ref=stat_all.at[flat], send_sem=stat_send,
-            recv_sem=stat_recv, device_id=device(d), device_id_type=MESH).start()
+            src_ref=stat_all.at[flat], dst_ref=stat_all.at[flat], send_sem=stat_send, recv_sem=stat_recv,
+            device_id={"client": client, "head": head}, device_id_type=MESH).start()
+    each_other(tell)
+
+    wait_all(part.at[pl.ds(0, zs * q * sub)], pair_send)
+    def line_sent(r, carry):
+        line_copy(r).wait_send()
         return carry
-    lax.fori_loop(1, devices, tell, 0)
-
-    wait_all(part.at[pl.ds(0, zs * q * sub)], pair_send)
-    for i in range(relays - queue, relays):
-        line_copy(i).wait_send()
+    lax.fori_loop(relays - queue, relays, line_sent, 0)
     wait_all(part.at[pl.ds(0, firsts * sub)], first_send)
     swap_copy.wait_send()
     embed_pair.wait_send()
@@ -650,8 +675,8 @@
             pltpu.VMEM((clients, emit), F32),
             pltpu.VMEM((padded, emit), F32),
             pltpu.VMEM((n * heads, 1, 128), F32),
-            dma((3,)), dma((rows // chunk,)), dma, dma,
-            dma, dma((zs * q,)), dma((3,)), dma(((zs + 1) * q,)),
+            dma((2,)), dma((rows // chunk,)), dma((rows // chunk,)), dma, dma,
+            dma, dma((zs * q,)), dma((4,)), dma(((zs + 1) * q,)),
             dma, dma(((zs + 1) * 2,)), dma((2,)), dma, dma,
             dma((2,)), dma((4,)), dma((2,)), dma, dma((2,)), dma((2,)), dma((2,)), dma((2,)), dma((zs,)),
             dma, dma, dma, dma, dma,

time: 105 us -> 102 us (0.971)
  Pallas kernels: 105 us -> 101 us
    pallas_call x1, Pallas kernels: 102 us -> 98.3 us  [per_device(): pl.pallas_call(functools.partial(kernel, cfg), out_shape=(jax.ShapeDtypeS...]
where the time goes in v5:
time: 102 us
  Pallas kernels  101 us (99%)
    pallas_call x1, Pallas kernels, per_device(): pl.pallas_call(functools.partial(kernel, cfg), out_shape=(jax.ShapeDtypeS...  98.3 us
    pallas_call x1, Pallas kernels, per_device(): pl.pallas_call(functools.partial(scale_kernel, sizes), out_shape=(jax.Sha...  2.7 us

profile of v5, /device:TPU:0, one launch (start us, length us, event | category | flops | bytes accessed | tf_op | source)
XLA Modules:
  0.0 101.7 jit_solution(3284062691717132925)
XLA Ops:
  0.6 98.3 %clipped_grads.1 = (f32[512,1024]{1,0:T(8,128)}, f32[96,1024]{1,0:T(8,128)}, f32[16,1024]{1,0:T(8,128)}, f32[1,128]{1,0:T(1,128)}) custom-call(bf16[1280,4096]{1,0:T(8,128)(2,1)} %pre_ref.1, f32[1280,1024]{1,0:T(8,128)} %delta_ref.1, bf16[4096,1024]{1,0:T(8,128)(2,1)} %weight_ref.1, s32[1,16]{1,0:T(1,128)} %bitcast.2), custom_call_target="tpu_custom_call" | custom-call | tf_op jit(solution)/shard_map/clipped_grads/pallas_call | solution.py:645
  99.0 2.7 %scaled.1 = (f32[512,1024]{1,0:T(8,128)}, f32[1,1024]{1,0:T(1,128)}, f32[16,1024]{1,0:T(8,128)}, f32[80,1024]{1,0:T(8,128)}) custom-call(f32[1,128]{1,0:T(1,128)} %get-tuple-element.12.stat_ref, f32[512,1024]{1,0:T(8,128)} %get-tuple-element.13.head_ref, f32[96,1024]{1,0:T(8,128)} %get-tuple-element.14.rest_ref, f32[16,1024]{1,0:T(8,128)} %get-tuple-element.15.embed_ref), custom_call_target="tpu_custom_call" | custom-call | tf_op jit(solution)/shard_map/scaled/pallas_call | solution.py:691

commit v6 on v5

--- a/solution.py
+++ b/solution.py
@@ -19,11 +19,11 @@
 
 
 def kernel(cfg, pre_ref, delta_ref, weight_ref, ids_ref, head_out, rest_out, embed_out, stat_out,
-           pre_v, delta_v, low, weight_v, part, pair_in, line_in, first_in, swap_in, head_v,
+           pre_v, delta_v, low, weight_v, part, pair_in, line_in, first_in, swap_in, cross_in, head_v,
            small, small_in, mine, span_in, span_part, span_pair, span_all, embed_all, ids_all,
            embed_v, rest_v, stat_all,
            pre_sem, first_pre_sem, delta_sem, weight_sem, out_sem, pair_send, pair_recv, line_send, line_recv,
-           first_send, first_recv, swap_sem, head_send, head_recv, span_send, span_recv, span_pair_sem,
+           first_send, first_recv, swap_sem, cross_sem, head_send, head_recv, span_send, span_recv, span_pair_sem,
            all_send, all_recv, write_sem, embed_pair_sem, embed_send, embed_recv, ids_sem, ids_send, ids_recv,
            stat_send, stat_recv):
     n, heads, block, piece, spans, clients = cfg
@@ -159,7 +159,9 @@
                     pair_send, pair_recv.at[i], partner)
 
     queue = 3 + middle
-    swaps = 1 if zs == 4 else 0
+    cross = zs == 4
+    swaps = 1 if cross else 0
+    skip = q - 1
 
     def order(r):
         m = r - q
@@ -168,7 +170,7 @@
 
     def pairs_sent(r):
         late = swaps * middle * ((r - q + relays) // relays)
-        return late * (2 * q + 2 + (r - q) // 2) + (1 - late) * (r + q + 2 * middle)
+        return late * (2 * q + 3 + (r - q) // 2) + (1 - late) * (r + q + (2 + swaps) * middle)
 
     def line_copy(r):
         i = order(r)
@@ -181,17 +183,32 @@
 
     def start_pairs(start, stop):
         def body(i, carry):
-            @pl.when(i < zs * q)
+            @pl.when((i < zs * q) & (swaps * middle * (skip + 1) != i + 1))
             def _():
                 pair_copy(i).start()
             return carry
         lax.fori_loop(start, stop, body, 0)
+
+    cross_copy = send(part.at[pl.ds(piece_row(dest(0), 1 - x, skip), sub), :], cross_in,
+                      cross_sem.at[0], cross_sem.at[1], landing(dest(0))[0])
+
+    def cross_add():
+        row = piece_row(dest(1), 1 - x, skip)
+        cross_copy.wait_recv()
+        def add(r, carry):
+            at = pl.ds(pl.multiple_of(r * step_rows, step_rows), step_rows)
+            mine_at = pl.ds(pl.multiple_of(row + r * step_rows, step_rows), step_rows)
+            part[mine_at, :] = (part[mine_at, :].astype(F32) + cross_in[at, :].astype(F32)).astype(BF16)
+            return carry
+        lax.fori_loop(0, sub // step_rows, add, 0)
 
     def relay(r, extra):
         i = order(r)
         place = dest(i // q)
         row = piece_row(place, x, i % q)
-        pair_copy(i).wait_recv()
+        @pl.when(swaps * middle * (skip + 1) != i + 1)
+        def _():
+            pair_copy(i).wait_recv()
         @pl.when(middle == 1)
         def _():
             wait_all(line_in.at[place * q + i % q], line_recv.at[place * q + i % q])
@@ -304,6 +321,7 @@
         pltpu.make_async_copy(head_v.at[pl.ds(0, sub), :], head_out.at[pl.ds(0, sub), :], out_sem).start()
         return square
 
+    opened = min(128, piece)
     lax.fori_loop(1, firsts, load, 0)
     step = 64
     for c in range(rows // chunk):
@@ -315,23 +333,32 @@
             return carry
         lax.fori_loop(0, chunk // step, narrow, 0)
         at = pl.ds(c * chunk, chunk)
-        p = pre_v[0, at, pl.ds(0, piece)].astype(F32)
+        p = pre_v[0, at, pl.ds(0, opened)].astype(F32)
         hidden = (p * jax.nn.sigmoid(p)).astype(BF16)
         value = lax.dot_general(hidden, low[at, :], (((0,), (0,)), ((), ())), preferred_element_type=F32)
         if c > 0:
-            value = value + head_v[pl.ds(0, piece), :]
+            value = value + head_v[pl.ds(0, opened), :]
         if c < len(delta_copies) - 1:
-            head_v[pl.ds(0, piece), :] = value
+            head_v[pl.ds(0, opened), :] = value
         else:
-            part[pl.ds(pl.multiple_of(unit_row(0), piece), piece), :] = value.astype(BF16)
+            part[pl.ds(pl.multiple_of(unit_row(0), opened), opened), :] = value.astype(BF16)
 
     pl.semaphore_wait(barrier, devices - 1)
 
-    ready = piece // sub - 1
+    ready = min(piece // sub - 1, q)
+    soon = min(opened // sub - 1, q)
     @pl.when(middle == 0)
     def _():
         first_copy(0).start()
-    for i in range(min(ready, q)):
+    for i in range(soon):
+        pair_copy(i).start()
+    if opened < piece:
+        rest = piece - opened
+        p = pre_v[0, :, pl.ds(opened, rest)].astype(F32)
+        hidden = (p * jax.nn.sigmoid(p)).astype(BF16)
+        value = lax.dot_general(hidden, low[...], (((0,), (0,)), ((), ())), preferred_element_type=F32)
+        part[pl.ds(pl.multiple_of(unit_row(0) + opened, opened), rest), :] = value.astype(BF16)
+    for i in range(soon, ready):
         pair_copy(i).start()
     lax.fori_loop(0 if hq > 1 else firsts, 2 * zs, load_rest, 0)
     weight_copy.start()
@@ -353,7 +380,12 @@
             product(t // (hq - 1), 1 + t % (hq - 1))
             return carry
         lax.fori_loop(0, 3 * (hq - 1), second, 0)
-    start_pairs(min(ready, q), pairs_sent(0))
+    if cross:
+        @pl.when(middle == 1)
+        def _():
+            pair_in[skip] = jnp.zeros((sub, emit), BF16)
+            cross_copy.start()
+    start_pairs(ready, pairs_sent(0))
     first_relay(0)
     first_relay(1)
     weight_copy.wait()
@@ -380,6 +412,11 @@
         pltpu.make_async_remote_copy(
             src_ref=small.at[target], dst_ref=small_in.at[lax.rem(my_head - target + heads, heads) - 1],
             send_sem=head_send, recv_sem=head_recv, device_id={"head": target}, device_id_type=MESH).start()
+
+    if cross:
+        @pl.when(middle == 1)
+        def _():
+            cross_add()
 
     done = slopes // 2
     if done < firsts:
@@ -553,7 +590,14 @@
             device_id={"client": client, "head": head}, device_id_type=MESH).start()
     each_other(tell)
 
-    wait_all(part.at[pl.ds(0, zs * q * sub)], pair_send)
+    @pl.when(swaps * middle == 0)
+    def _():
+        wait_all(part.at[pl.ds(0, zs * q * sub)], pair_send)
+    if cross:
+        @pl.when(middle == 1)
+        def _():
+            wait_all(part.at[pl.ds(0, (zs * q - 1) * sub)], pair_send)
+            cross_copy.wait_send()
     def line_sent(r, carry):
         line_copy(r).wait_send()
         return carry
@@ -595,20 +639,16 @@
     def part(ref, i):
         return ref.at[pl.ds(i * rows, rows), :]
     stat_in.start()
+    rest_in.start()
+    embed_in.start()
     heads_in = [pltpu.make_async_copy(part(head_ref, i), part(head, i), in_sem.at[i]) for i in range(steps)]
     heads_out = [pltpu.make_async_copy(part(head, i), part(head_out, i), out_sem.at[i]) for i in range(steps)]
     for copy in heads_in:
         copy.start()
-    rest_in.start()
-    embed_in.start()
     stat_in.wait()
     factor = clip_factor(stat[0:1, 0:1], head_size)
     embed_factor = clip_factor(stat[0:1, 1:2], embed_size)
     rest_factor = clip_factor(stat[0:1, 2:3], rest_size)
-    for i in range(steps):
-        heads_in[i].wait()
-        head[pl.ds(i * rows, rows), :] = factor * head[pl.ds(i * rows, rows), :]
-        heads_out[i].start()
     rest_in.wait()
     rest[...] = rest_factor * rest[...]
     bias_copy = pltpu.make_async_copy(rest.at[pl.ds(spans, 1), :], bias_out, out_sem.at[steps])
@@ -619,6 +659,10 @@
     embed[...] = embed_factor * embed[...]
     embed_copy = pltpu.make_async_copy(embed, embed_out, out_sem.at[steps + 2])
     embed_copy.start()
+    for i in range(steps):
+        heads_in[i].wait()
+        head[pl.ds(i * rows, rows), :] = factor * head[pl.ds(i * rows, rows), :]
+        heads_out[i].start()
     for copy in heads_out + [bias_copy, span_copy, embed_copy]:
         copy.wait()
 
@@ -662,6 +706,7 @@
             pltpu.VMEM(((zs + 2) * q, sub, emit), BF16),
             pltpu.VMEM(((zs + 2) * 2, sub, emit), BF16),
             pltpu.VMEM((sub, emit), BF16),
+            pltpu.VMEM((sub, emit), BF16),
             pltpu.VMEM((block, emit), F32),
             pltpu.VMEM((heads, spans + clients, emit), BF16),
             pltpu.VMEM((heads - 1, spans + clients, emit), BF16),
@@ -677,7 +722,7 @@
             pltpu.VMEM((n * heads, 1, 128), F32),
             dma((2,)), dma((rows // chunk,)), dma((rows // chunk,)), dma, dma,
             dma, dma((zs * q,)), dma((4,)), dma(((zs + 1) * q,)),
-            dma, dma(((zs + 1) * 2,)), dma((2,)), dma, dma,
+            dma, dma(((zs + 1) * 2,)), dma((2,)), dma((2,)), dma, dma,
             dma((2,)), dma((4,)), dma((2,)), dma, dma((2,)), dma((2,)), dma((2,)), dma((2,)), dma((zs,)),
             dma, dma, dma, dma, dma,
         ],

time: 102 us -> 101 us (level)
  Pallas kernels: 101 us -> 99.8 us
    pallas_call x1, Pallas kernels: 98.3 us -> 97.1 us  [per_device(): pl.pallas_call(functools.partial(kernel, cfg), out_shape=(jax.ShapeDtypeS...]
where the time goes in v6:
time: 101 us; the launch traced here: 100 us
  Pallas kernels  99.8 us (99%)
    pallas_call x1, Pallas kernels, per_device(): pl.pallas_call(functools.partial(kernel, cfg), out_shape=(jax.ShapeDtypeS...  97.1 us
    pallas_call x1, Pallas kernels, per_device(): pl.pallas_call(functools.partial(scale_kernel, sizes), out_shape=(jax.Sha...  2.74 us

profile of v6, /device:TPU:0, one launch (start us, length us, event | category | flops | bytes accessed | tf_op | source)
XLA Modules:
  0.0 100.4 jit_solution(5975732905384025551)
XLA Ops:
  0.6 97.1 %clipped_grads.1 = (f32[512,1024]{1,0:T(8,128)}, f32[96,1024]{1,0:T(8,128)}, f32[16,1024]{1,0:T(8,128)}, f32[1,128]{1,0:T(1,128)}) custom-call(bf16[1280,4096]{1,0:T(8,128)(2,1)} %pre_ref.1, f32[1280,1024]{1,0:T(8,128)} %delta_ref.1, bf16[4096,1024]{1,0:T(8,128)(2,1)} %weight_ref.1, s32[1,16]{1,0:T(1,128)} %bitcast.2), custom_call_target="tpu_custom_call" | custom-call | tf_op jit(solution)/shard_map/clipped_grads/pallas_call | solution.py:689
  97.7 2.7 %scaled.1 = (f32[512,1024]{1,0:T(8,128)}, f32[1,1024]{1,0:T(1,128)}, f32[16,1024]{1,0:T(8,128)}, f32[80,1024]{1,0:T(8,128)}) custom-call(f32[1,128]{1,0:T(1,128)} %get-tuple-element.12.stat_ref, f32[512,1024]{1,0:T(8,128)} %get-tuple-element.13.head_ref, f32[96,1024]{1,0:T(8,128)} %get-tuple-element.14.rest_ref, f32[16,1024]{1,0:T(8,128)} %get-tuple-element.15.embed_ref), custom_call_target="tpu_custom_call" | custom-call | tf_op jit(solution)/shard_map/scaled/pallas_call | solution.py:736

commit v7 on v6

--- a/solution.py
+++ b/solution.py
@@ -19,10 +19,10 @@
 
 
 def kernel(cfg, pre_ref, delta_ref, weight_ref, ids_ref, head_out, rest_out, embed_out, stat_out,
-           pre_v, delta_v, low, weight_v, part, pair_in, line_in, first_in, swap_in, cross_in, head_v,
+           pre_v, delta_v, low, weight_v, part, pair_in, line_in, first_in, swap_in, cross_in, sum_v, head_v,
            small, small_in, mine, span_in, span_part, span_pair, span_all, embed_all, ids_all,
            embed_v, rest_v, stat_all,
-           pre_sem, first_pre_sem, delta_sem, weight_sem, out_sem, pair_send, pair_recv, line_send, line_recv,
+           pre_sem, delta_sem, weight_sem, out_sem, pair_send, pair_recv, line_send, line_recv,
            first_send, first_recv, swap_sem, cross_sem, head_send, head_recv, span_send, span_recv, span_pair_sem,
            all_send, all_recv, write_sem, embed_pair_sem, embed_send, embed_recv, ids_sem, ids_send, ids_recv,
            stat_send, stat_recv):
@@ -97,25 +97,32 @@
         for c in range(rows // chunk)]
     weight_copy = pltpu.make_async_copy(weight_ref, weight_v, weight_sem)
     ids_copy = pltpu.make_async_copy(ids_ref, ids_all.at[me], ids_sem)
-    first_column = pl.multiple_of(unit_row(0), piece)
+    opened = min(128, piece)
+    first_column = pl.multiple_of(unit_row(0), opened)
+    rest_columns = piece - opened
+    rest_copy = None
+    if rest_columns > 0:
+        rest_copy = pltpu.make_async_copy(
+            pre_ref.at[:, pl.ds(pl.multiple_of(first_column + opened, opened), rest_columns)],
+            pre_v.at[0, :, pl.ds(opened, rest_columns)], pre_sem.at[2])
     first_copies = [
-        pltpu.make_async_copy(pre_ref.at[pl.ds(c * chunk, chunk), pl.ds(first_column, piece)],
-                              pre_v.at[0, pl.ds(c * chunk, chunk), pl.ds(0, piece)], first_pre_sem.at[c])
+        pltpu.make_async_copy(pre_ref.at[pl.ds(c * chunk, chunk), pl.ds(first_column, opened)],
+                              pre_v.at[0, pl.ds(c * chunk, chunk), pl.ds(0, opened)], delta_sem.at[c])
         for c in range(rows // chunk)]
     for c in range(rows // chunk):
         first_copies[c].start()
         delta_copies[c].start()
 
     def each_other(action):
-        columns = [lax.rem(my_head + d, heads) for d in range(heads)]
-        for column in columns[1:]:
-            action(me, column)
-        def body(d, carry):
-            client = lax.rem(me + d, n)
+        columns = [lax.rem(my_head + d, heads) for d in range(heads - 1, -1, -1)]
+        def body(j, carry):
+            client = dest(j // 2) * 2 + unit_side(j)
             for column in columns:
                 action(client, column)
             return carry
-        lax.fori_loop(1, n, body, 0)
+        lax.fori_loop(0, n - 1, body, 0)
+        for column in columns[:-1]:
+            action(me, column)
 
     barrier = pltpu.get_barrier_semaphore()
     def greet(client, head):
@@ -250,7 +257,7 @@
             out_at = pl.ds(pl.multiple_of((s + 1) * sub + r * step_rows, step_rows), step_rows)
             total = part[mine_at, :].astype(F32) + pair_in[i, at, :].astype(F32)
             total = total + line_in[left, at, :].astype(F32) + line_in[right, at, :].astype(F32)
-            head_v[out_at, :] = total
+            head_v[out_at, :] = total.astype(BF16)
             return carry + jnp.sum((total * total).reshape(step_rows // 8, 8, emit), axis=0)
         square = lax.fori_loop(0, sub // step_rows, add, square)
         at = pl.ds(pl.multiple_of((s + 1) * sub, sub), sub)
@@ -315,18 +322,18 @@
             mine_at = pl.ds(pl.multiple_of(row + r * step_rows, step_rows), step_rows)
             total = part[mine_at, :].astype(F32) + first_in[left, at, :].astype(F32)
             total = total + first_in[right, at, :].astype(F32) + swap_in[at, :].astype(F32)
-            head_v[at, :] = total
+            head_v[at, :] = total.astype(BF16)
             return carry + jnp.sum((total * total).reshape(step_rows // 8, 8, emit), axis=0)
         square = lax.fori_loop(0, sub // step_rows, add, square)
         pltpu.make_async_copy(head_v.at[pl.ds(0, sub), :], head_out.at[pl.ds(0, sub), :], out_sem).start()
         return square
 
-    opened = min(128, piece)
+    if rest_columns > 0:
+        rest_copy.start()
     lax.fori_loop(1, firsts, load, 0)
     step = 64
     for c in range(rows // chunk):
-        first_copies[c].wait()
-        delta_copies[c].wait()
+        wait_all(delta_v.at[pl.ds(0, chunk + chunk * opened // (2 * emit)), :], delta_sem.at[c])
         def narrow(r, carry):
             at = pl.ds(pl.multiple_of(c * chunk + r * step, step), step)
             low[at, :] = delta_v[at, :].astype(BF16)
@@ -337,9 +344,9 @@
         hidden = (p * jax.nn.sigmoid(p)).astype(BF16)
         value = lax.dot_general(hidden, low[at, :], (((0,), (0,)), ((), ())), preferred_element_type=F32)
         if c > 0:
-            value = value + head_v[pl.ds(0, opened), :]
+            value = value + sum_v[...]
         if c < len(delta_copies) - 1:
-            head_v[pl.ds(0, opened), :] = value
+            sum_v[...] = value
         else:
             part[pl.ds(pl.multiple_of(unit_row(0), opened), opened), :] = value.astype(BF16)
 
@@ -352,12 +359,12 @@
         first_copy(0).start()
     for i in range(soon):
         pair_copy(i).start()
-    if opened < piece:
-        rest = piece - opened
-        p = pre_v[0, :, pl.ds(opened, rest)].astype(F32)
+    if rest_columns > 0:
+        rest_copy.wait()
+        p = pre_v[0, :, pl.ds(opened, rest_columns)].astype(F32)
         hidden = (p * jax.nn.sigmoid(p)).astype(BF16)
         value = lax.dot_general(hidden, low[...], (((0,), (0,)), ((), ())), preferred_element_type=F32)
-        part[pl.ds(pl.multiple_of(unit_row(0) + opened, opened), rest), :] = value.astype(BF16)
+        part[pl.ds(pl.multiple_of(unit_row(0) + opened, opened), rest_columns), :] = value.astype(BF16)
     for i in range(soon, ready):
         pair_copy(i).start()
     lax.fori_loop(0 if hq > 1 else firsts, 2 * zs, load_rest, 0)
@@ -628,7 +635,7 @@
 
 
 def scale_kernel(sizes, stat_ref, head_ref, rest_ref, embed_ref, head_out, bias_out, embed_out, span_out,
-                 stat, head, rest, embed, in_sem, out_sem):
+                 stat, head_in, head, rest, embed, in_sem, out_sem):
     head_size, embed_size, rest_size = sizes
     spans = span_out.shape[0]
     steps = in_sem.shape[0] - 3
@@ -639,16 +646,20 @@
     def part(ref, i):
         return ref.at[pl.ds(i * rows, rows), :]
     stat_in.start()
-    rest_in.start()
-    embed_in.start()
-    heads_in = [pltpu.make_async_copy(part(head_ref, i), part(head, i), in_sem.at[i]) for i in range(steps)]
+    heads_in = [pltpu.make_async_copy(part(head_ref, i), part(head_in, i), in_sem.at[i]) for i in range(steps)]
     heads_out = [pltpu.make_async_copy(part(head, i), part(head_out, i), out_sem.at[i]) for i in range(steps)]
     for copy in heads_in:
         copy.start()
+    rest_in.start()
+    embed_in.start()
     stat_in.wait()
     factor = clip_factor(stat[0:1, 0:1], head_size)
     embed_factor = clip_factor(stat[0:1, 1:2], embed_size)
     rest_factor = clip_factor(stat[0:1, 2:3], rest_size)
+    for i in range(steps):
+        heads_in[i].wait()
+        head[pl.ds(i * rows, rows), :] = factor * head_in[pl.ds(i * rows, rows), :].astype(F32)
+        heads_out[i].start()
     rest_in.wait()
     rest[...] = rest_factor * rest[...]
     bias_copy = pltpu.make_async_copy(rest.at[pl.ds(spans, 1), :], bias_out, out_sem.at[steps])
@@ -659,10 +670,6 @@
     embed[...] = embed_factor * embed[...]
     embed_copy = pltpu.make_async_copy(embed, embed_out, out_sem.at[steps + 2])
     embed_copy.start()
-    for i in range(steps):
-        heads_in[i].wait()
-        head[pl.ds(i * rows, rows), :] = factor * head[pl.ds(i * rows, rows), :]
-        heads_out[i].start()
     for copy in heads_out + [bias_copy, span_copy, embed_copy]:
         copy.wait()
 
@@ -689,7 +696,7 @@
     head_raw, rest_raw, embed_raw, stats = pl.pallas_call(
         functools.partial(kernel, cfg),
         out_shape=(
-            jax.ShapeDtypeStruct((block, emit), F32),
+            jax.ShapeDtypeStruct((block, emit), BF16),
             jax.ShapeDtypeStruct((padded, emit), F32),
             jax.ShapeDtypeStruct((clients, emit), F32),
             jax.ShapeDtypeStruct((1, 128), F32),
@@ -707,7 +714,8 @@
             pltpu.VMEM(((zs + 2) * 2, sub, emit), BF16),
             pltpu.VMEM((sub, emit), BF16),
             pltpu.VMEM((sub, emit), BF16),
-            pltpu.VMEM((block, emit), F32),
+            pltpu.VMEM((min(128, piece), emit), F32),
+            pltpu.VMEM((block, emit), BF16),
             pltpu.VMEM((heads, spans + clients, emit), BF16),
             pltpu.VMEM((heads - 1, spans + clients, emit), BF16),
             pltpu.VMEM((2, padded, half), BF16),
@@ -720,7 +728,7 @@
             pltpu.VMEM((clients, emit), F32),
             pltpu.VMEM((padded, emit), F32),
             pltpu.VMEM((n * heads, 1, 128), F32),
-            dma((2,)), dma((rows // chunk,)), dma((rows // chunk,)), dma, dma,
+            dma((3,)), dma((rows // chunk,)), dma, dma,
             dma, dma((zs * q,)), dma((4,)), dma(((zs + 1) * q,)),
             dma, dma(((zs + 1) * 2,)), dma((2,)), dma((2,)), dma, dma,
             dma((2,)), dma((4,)), dma((2,)), dma, dma((2,)), dma((2,)), dma((2,)), dma((2,)), dma((zs,)),
@@ -745,6 +753,7 @@
         out_specs=(hbm,) * 4,
         scratch_shapes=[
             pltpu.VMEM((1, 128), F32),
+            pltpu.VMEM((block, emit), BF16),
             pltpu.VMEM((block, emit), F32),
             pltpu.VMEM((padded, emit), F32),
             pltpu.VMEM((clients, emit), F32),

time: 101 us -> 100 us (0.990)
  no operation moved by 1% of the time
where the time goes in v7:
time: 100 us
  Pallas kernels  99.5 us (100%)
    pallas_call x1, Pallas kernels, per_device(): pl.pallas_call(functools.partial(kernel, cfg), out_shape=(jax.ShapeDtypeS...  96.9 us
    pallas_call x1, Pallas kernels, per_device(): pl.pallas_call(functools.partial(scale_kernel, sizes), out_shape=(jax.Sha...  2.61 us

profile of v7, /device:TPU:0, one launch (start us, length us, event | category | flops | bytes accessed | tf_op | source)
XLA Modules:
  0.0 100.2 jit_solution(14068430549147955144)
XLA Ops:
  0.6 96.9 %clipped_grads.1 = (bf16[512,1024]{1,0:T(8,128)(2,1)}, f32[96,1024]{1,0:T(8,128)}, f32[16,1024]{1,0:T(8,128)}, f32[1,128]{1,0:T(1,128)}) custom-call(bf16[1280,4096]{1,0:T(8,128)(2,1)} %pre_ref.1, f32[1280,1024]{1,0:T(8,128)} %delta_ref.1, bf16[4096,1024]{1,0:T(8,128)(2,1)} %weight_ref.1, s32[1,16]{1,0:T(1,128)} %bitcast.2), custom_call_target="tpu_custom_call" | custom-call | tf_op jit(solution)/shard_map/clipped_grads/pallas_call | solution.py:696
  97.6 2.6 %scaled.1 = (f32[512,1024]{1,0:T(8,128)}, f32[1,1024]{1,0:T(1,128)}, f32[16,1024]{1,0:T(8,128)}, f32[80,1024]{1,0:T(8,128)}) custom-call(f32[1,128]{1,0:T(1,128)} %get-tuple-element.12.stat_ref, bf16[512,1024]{1,0:T(8,128)(2,1)} %get-tuple-element.13.head_ref, f32[96,1024]{1,0:T(8,128)} %get-tuple-element.14.rest_ref, f32[16,1024]{1,0:T(8,128)} %get-tuple-element.15.embed_ref), custom_call_target="tpu_custom_call" | custom-call | tf_op jit(solution)/shard_map/scaled/pallas_call | solution.py:744

commit v8 on v7

--- a/solution.py
+++ b/solution.py
@@ -120,7 +120,8 @@
             for column in columns:
                 action(client, column)
             return carry
-        lax.fori_loop(0, n - 1, body, 0)
+        for j in range(n - 1):
+            body(j, 0)
         for column in columns[:-1]:
             action(me, column)
 
@@ -186,7 +187,7 @@
         return send(part.at[pl.ds(piece_row(place, x, i % q), sub), :], line_in.at[slot * q + i % q],
                     line_send.at[r % queue], line_recv.at[sem * q + i % q], target)
 
-    step_rows = min(32, sub)
+    step_rows = min(64, sub)
 
     def start_pairs(start, stop):
         def body(i, carry):
@@ -740,7 +741,7 @@
         name="clipped_grads",
     )(pre, delta, head_weight, ids)
     sizes = (hidden_width * emit * heads, clients * n * hidden_width, spans * hidden_width + emit * heads)
-    steps = 4
+    steps = 2
     head_grad, bias_grad, embed_grad, span_grad = pl.pallas_call(
         functools.partial(scale_kernel, sizes),
         out_shape=(

time: 100 us -> 100 us (level)
  no operation moved by 1% of the time
where the time goes in v8:
time: 100 us
  Pallas kernels  99.6 us (100%)
    pallas_call x1, Pallas kernels, per_device(): pl.pallas_call(functools.partial(kernel, cfg), out_shape=(jax.ShapeDtypeS...  96.9 us
    pallas_call x1, Pallas kernels, per_device(): pl.pallas_call(functools.partial(scale_kernel, sizes), out_shape=(jax.Sha...  2.7 us

profile of v8, /device:TPU:0, one launch (start us, length us, event | category | flops | bytes accessed | tf_op | source)
XLA Modules:
  0.0 100.2 jit_solution(5414874008339793620)
XLA Ops:
  0.6 96.9 %clipped_grads.1 = (bf16[512,1024]{1,0:T(8,128)(2,1)}, f32[96,1024]{1,0:T(8,128)}, f32[16,1024]{1,0:T(8,128)}, f32[1,128]{1,0:T(1,128)}) custom-call(bf16[1280,4096]{1,0:T(8,128)(2,1)} %pre_ref.1, f32[1280,1024]{1,0:T(8,128)} %delta_ref.1, bf16[4096,1024]{1,0:T(8,128)(2,1)} %weight_ref.1, s32[1,16]{1,0:T(1,128)} %bitcast.2), custom_call_target="tpu_custom_call" | custom-call | tf_op jit(solution)/shard_map/clipped_grads/pallas_call | solution.py:697
  97.5 2.7 %scaled.1 = (f32[512,1024]{1,0:T(8,128)}, f32[1,1024]{1,0:T(1,128)}, f32[16,1024]{1,0:T(8,128)}, f32[80,1024]{1,0:T(8,128)}) custom-call(f32[1,128]{1,0:T(1,128)} %get-tuple-element.12.stat_ref, bf16[512,1024]{1,0:T(8,128)(2,1)} %get-tuple-element.13.head_ref, f32[96,1024]{1,0:T(8,128)} %get-tuple-element.14.rest_ref, f32[16,1024]{1,0:T(8,128)} %get-tuple-element.15.embed_ref), custom_call_target="tpu_custom_call" | custom-call | tf_op jit(solution)/shard_map/scaled/pallas_call | solution.py:745
